TPU v7x, 128 devices: a whole 4x4x4 slice. The times are simulated.
128 devices in a mesh: fc: 16 (over z, y_lo, core), tok: 8 (over x, y_hi).
Axes of the slice: x: 4, y: 4 (y_hi: 2, y_lo: 2; y = y_hi * 2 + y_lo), z: 4, core: 2. Of those that a mesh axis runs over, the one named last changes fastest.
Arguments:
- tokens: bfloat16 [16, 64, 128, 1024], P('fc', 'tok'), may hold values from -6 to 6
- slot_keys: bfloat16 [1024, 1024], replicated, may hold values from -2 to 2
- norm_gain: float32 [1024], replicated, may hold values from 0.25 to 1.75
- slot_gain: float32 [1024], replicated, may hold values from 0.25 to 1.75
- w_in: bfloat16 [256, 1024, 512], P(('fc', 'tok')), may hold values from -0.1875 to 0.1875
- w_out: bfloat16 [256, 512, 1024], P(('fc', 'tok')), may hold values from -0.25 to 0.25
- conv_weight: float32 [7, 7, 1024], replicated, may hold values from -0.875 to 0.875
- ln_gain: float32 [1024], replicated, may hold values from 0.25 to 1.75
- proj: bfloat16 [1024, 1024], replicated, may hold values from -0.1875 to 0.1875
- layer_scale: float32 [1024], replicated, may hold values from 0.25 to 1.75
Outputs:
- fields: bfloat16 [16, 64, 128, 1024], P('fc', 'tok')
All inputs are finite; a program needn't handle non-finite values.
Results may differ from a plain program's by a relative error of at most 0.008.
The roundings to bfloat16 on the way count: a program that leaves them out, or rounds other values in their place, can miss the bound.
Values may be sent and summed in bfloat16 or wider, within the bound.
A program may use at most 64 MiB of HBM per device.

v0:
```python
import jax
import jax.numpy as jnp
from jax import lax
from jax.sharding import Mesh
from jax.sharding import PartitionSpec as P

TOK = ("tok_0", "tok_1")
FC_TOK = ("fc", "tok_0", "tok_1")


def from_everyone(x, axis):
    size = lax.axis_size(axis)
    return lax.all_to_all(jnp.broadcast_to(x[None], (size, *x.shape)), axis, 0, 0, tiled=True)


def of_everyone(x, axis):
    return from_everyone(x, axis).max(axis=0)


def summed_rows(x, axes, dim):
    for axis in axes:
        x = lax.psum_scatter(x, axis, scatter_dimension=dim, tiled=True)
    return x


def joined_along(pieces, dim):
    pieces = jnp.moveaxis(pieces, 0, dim)
    dims = pieces.shape
    return pieces.reshape(*dims[:dim], dims[dim] * dims[dim + 1], *dims[dim + 2 :])


def gathered_copies(x, axis, dim):
    return joined_along(from_everyone(x, axis), dim)


def with_halo(block, sides, width):
    for axis, dim in sides:
        count = lax.axis_size(axis)
        forward = [(i, i + 1) for i in range(count - 1)]
        backward = [(target, source) for source, target in forward]
        low = lax.ppermute(
            lax.slice_in_dim(block, block.shape[dim] - width, None, axis=dim), axis, forward
        )
        high = lax.ppermute(lax.slice_in_dim(block, 0, width, axis=dim), axis, backward)
        block = jnp.concatenate([low, block, high], axis=dim)
    return block


def rms_scale(value, gain):
    return value * lax.rsqrt(jnp.mean(value * value, axis=-1, keepdims=True) + 1e-06) * gain


def local(
    tokens, slot_keys, norm_gain, slot_gain, w_in, w_out, conv_weight, ln_gain, proj, layer_scale
):
    rows = tokens.shape[1]
    cols = tokens.shape[2]
    width = tokens.shape[3]
    count_fc = lax.axis_size("fc")
    count_tok = lax.axis_size(TOK)
    slot_total = slot_keys.shape[1]
    slot_dev = slot_total // (count_fc * count_tok)
    cells = tokens.reshape(rows * cols, width)
    normed = rms_scale(cells.astype(jnp.float32), norm_gain).astype(jnp.bfloat16)
    logits = jnp.dot(normed, slot_keys, preferred_element_type=jnp.float32)
    peak = of_everyone(jnp.max(logits, axis=0), TOK)
    shifted = jnp.exp(logits - peak)
    dispatch = shifted.astype(jnp.bfloat16)
    numer = lax.dot_general(
        dispatch, cells, (((0,), (0,)), ((), ())), preferred_element_type=jnp.float32
    )
    numer = numer.reshape(count_fc, count_tok * slot_dev, width)
    numer = summed_rows(numer.astype(jnp.bfloat16), TOK, 1).astype(jnp.float32)
    local_in = rms_scale(numer, slot_gain).astype(jnp.bfloat16)
    slot_in = lax.all_to_all(local_in, "fc", split_axis=0, concat_axis=0, tiled=True)
    grouped = slot_in.reshape(count_fc, w_in.shape[0], slot_dev // w_in.shape[0], width)
    hidden = jax.nn.gelu(
        jnp.einsum("mesd,edf->mesf", grouped, w_in, preferred_element_type=jnp.float32)
    ).astype(jnp.bfloat16)
    expert_out = jnp.einsum(
        "mesf,efd->mesd", hidden, w_out, preferred_element_type=jnp.float32
    ).astype(jnp.bfloat16)
    expert_out = expert_out.reshape(count_fc, slot_dev, width)
    returned = lax.all_to_all(expert_out, "fc", split_axis=0, concat_axis=0, tiled=True)
    every_slot = gathered_copies(returned, TOK, 1).reshape(slot_total, width)
    combine = jax.nn.softmax(logits, axis=-1).astype(jnp.bfloat16)
    mixed = jnp.dot(combine, every_slot, preferred_element_type=jnp.float32)
    state = (cells.astype(jnp.float32) + mixed).astype(jnp.bfloat16).reshape(rows, cols, width)
    padded = with_halo(state, ((TOK, 0),), 3)
    padded = jnp.concatenate([padded[:, cols - 3 :], padded, padded[:, :3]], axis=1)
    conv = jnp.zeros((rows, cols, width), jnp.float32)
    for row_tap in range(7):
        for col_tap in range(7):
            conv = (
                conv
                + padded[row_tap : row_tap + rows, col_tap : col_tap + cols].astype(jnp.float32)
                * conv_weight[row_tap, col_tap]
            )
    center = conv - jnp.mean(conv, axis=-1, keepdims=True)
    spread = jnp.mean(center * center, axis=-1, keepdims=True)
    normal = (center * lax.rsqrt(spread + 1e-06) * ln_gain).astype(jnp.bfloat16)
    branch = jnp.dot(normal.reshape(rows * cols, width), proj, preferred_element_type=jnp.float32)
    result = state.reshape(rows * cols, width).astype(jnp.float32) + layer_scale * jax.nn.gelu(
        branch
    )
    return result.astype(jnp.bfloat16).reshape(1, rows, cols, width)


def solution(mesh):
    finer = Mesh(mesh.devices.reshape(mesh.shape["fc"], 4, 2), ("fc", "tok_0", "tok_1"))
    in_specs = (
        P("fc", TOK, None, None),
        P(),
        P(),
        P(),
        P(FC_TOK, None, None),
        P(FC_TOK, None, None),
        P(),
        P(),
        P(),
        P(),
    )
    out_specs = P("fc", TOK, None, None)
    return jax.shard_map(local, mesh=finer, in_specs=in_specs, out_specs=out_specs, check_vma=False)
```

profile of v0, /device:TPU:0, one launch (start us, length us, event | category | flops | bytes accessed | tf_op | source)
XLA Modules:
  0.0 239.6 jit_solution(7497052977742484070)
XLA Ops:
  6.5 0.0 copy-start
  6.5 0.0 reduce-scatter.5.cloned.1.call-start
  6.5 2.2 multiply_reduce_fusion.1
  8.8 0.0 copy-done
  8.8 4.1 %fusion.65 = (f32[1024]{0:T(1024)S(1)}, f32[1024,1024]{0,1:T(8,128)S(1)}) fusion(bf16[1024,1024]{1,0:T(8,128)(2,1)S(1)} %copy-done, bf16[1024,1024]{1,0:T(8,128)(2,1)} %bitcast.120, f32[1024]{0:T(1024)} %param.12, f32[1024]{0:T(1024)S(1)} %rsqrt_bitcast_fusion), kind=kOutput, calls=%fused_computation.87 | convolution fusion | flops 2152725504 | bytes 8400896 | tf_op jit(solution)/shard_map/dot_general | solution.py:65
  12.9 0.0 copy-start.1
  12.9 1.9 copy-done.1
  14.8 0.8 fusion.15
  15.6 14.6 %all_to_all.21 = f32[8,1,1024]{2,1,0:T(1,128)S(1)} all-to-all(f32[8,1,1024]{2,1,0:T(1,128)S(1)} %broadcast_in_dim.4), channel_id=1, replica_groups=mesh['fc'=16,'tok_0'=4,'tok_1'=2] {'tok_0','tok_1'}, dimensions={0} | all-to-all | bytes 65536 | tf_op jit(solution)/shard_map/all_to_all | solution.py:13
  30.2 0.0 copy-start.3
  30.2 2.9 %exponential_convert_fusion = bf16[1024,1024]{0,1:T(8,128)(2,1)S(1)} fusion(f32[1024,1024]{0,1:T(8,128)} %copy-done.1, f32[1024]{0:T(1024)S(1)} %reduce_max.29), kind=kLoop, calls=%fused_computation.19 | loop fusion | flops 2097152 | bytes 6295552 | tf_op jit(solution)/shard_map/convert_element_type | solution.py:68
  33.1 0.0 copy-done.3
  33.1 3.7 %convolution_convert_fusion = bf16[16,64,1024]{2,1,0:T(8,128)(2,1)} fusion(bf16[16,64,1024]{2,1,0:T(8,128)(2,1)S(1)} %bitcast.125, bf16[1024,1024,1]{1,0,2:T(8,128)(2,1)S(1)} %bitcast.121), kind=kOutput, calls=%fused_computation.52 | convolution fusion | flops 2148532224 | bytes 6291456 | tf_op jit(solution)/shard_map/dot_general | solution.py:69
  36.8 0.0 copy-start.6
  36.8 0.0 reduce-scatter.5.cloned.1.call-update
  36.8 0.0 reduce-scatter.7.cloned.1.call-start
  36.9 27.9 %reduce-scatter.5.cloned.1.call-done = bf16[16,16,1024]{2,1,0:T(8,128)(2,1)} async-done(((bf16[16,64,1024]{2,1,0:T(8,128)(2,1)}), bf16[16,16,1024]{2,1,0:T(8,128)(2,1)}) %reduce-scatter.5.cloned.1.call-update) | async-done | bytes 524304 | tf_op jit(solution)/shard_map/reduce_scatter | solution.py:22
  64.8 1.9 copy.30
  66.6 0.0 reduce-scatter.7.cloned.1.call-update
  66.7 18.9 %reduce-scatter.7.cloned.1.call-done = bf16[8,16384]{1,0:T(8,128)(2,1)} async-done(((bf16[16,16384]{1,0:T(8,128)(2,1)}), bf16[8,16384]{1,0:T(8,128)(2,1)}) %reduce-scatter.7.cloned.1.call-update) | async-done | bytes 262160
  85.6 1.1 copy.36
  86.7 0.2 fusion.35
  86.9 0.0 copy-done.6
  86.9 0.2 fusion.37
  87.1 12.4 %all_to_all.22 = bf16[16,8,1024]{2,1,0:T(8,128)(2,1)S(1)} all-to-all(bf16[16,8,1024]{2,1,0:T(8,128)(2,1)S(1)} %fusion.37), channel_id=1, replica_groups=mesh['fc'=16,'tok_0'=4,'tok_1'=2] {'fc'}, dimensions={0} | all-to-all | bytes 524288 | tf_op jit(solution)/shard_map/all_to_all | solution.py:75
  99.5 0.1 copy.22
  99.6 3.1 %fusion.29 = bf16[2,16,4,1024]{3,1,2,0:T(8,128)(2,1)S(1)} fusion(bf16[2,512,1024]{2,1,0:T(8,128)(2,1)} %param.15, bf16[16,2,4,1024]{3,0,2,1:T(8,128)(2,1)S(1)} %bitcast.126, bf16[2,1024,512]{2,1,0:T(8,128)(2,1)} %param.14), kind=kOutput, calls=%fused_computation.53 | convolution fusion | flops 269156352 | bytes 4718592 | tf_op jit(solution)/shard_map/mesf,efd->mesd/dot_general | solution.py:80
  102.7 0.2 copy.23
  102.9 10.6 %all_to_all.23 = bf16[16,8,1024]{2,1,0:T(8,128)(2,1)S(1)} all-to-all(bf16[16,8,1024]{2,1,0:T(8,128)(2,1)S(1)} %copy.23), channel_id=1, replica_groups=mesh['fc'=16,'tok_0'=4,'tok_1'=2] {'fc'}, dimensions={0} | all-to-all | bytes 524288 | tf_op jit(solution)/shard_map/all_to_all | solution.py:84
  113.5 0.3 broadcast_in_dim.5
  113.8 0.0 copy-start.2
  113.8 0.0 copy-start.4
  113.8 33.6 %all_to_all.24 = bf16[8,16,8,1024]{3,2,1,0:T(8,128)(2,1)S(1)} all-to-all(bf16[8,16,8,1024]{3,2,1,0:T(8,128)(2,1)S(1)} %broadcast_in_dim.5), channel_id=1, replica_groups=mesh['fc'=16,'tok_0'=4,'tok_1'=2] {'tok_0','tok_1'}, dimensions={0} | all-to-all | bytes 4194304 | tf_op jit(solution)/shard_map/all_to_all | solution.py:13
  147.4 0.2 copy.24
  147.5 0.0 copy-done.2
  147.5 0.0 copy-done.4
  147.6 0.0 copy-start.5
  147.6 2.4 %fusion.2 = bf16[1024,1024]{1,0:T(8,128)(2,1)S(1)} fusion(bf16[1,8,128,1024]{3,2,1,0:T(8,128)(2,1)S(1)} %copy-done.4, bf16[1024,1024]{1,0:T(8,128)(2,1)S(1)} %bitcast.122, f32[1024,1024]{0,1:T(8,128)S(1)} %copy-done.2, f32[1024]{0:T(1024)S(1)} %get-tuple-element.5, f32[1024]{0:T(1024)S(1)} %get-tuple-element.62), kind=kOutput, calls=%fused_computation.5 | convolution fusion | flops 2153775104 | bytes 10493952 | tf_op jit(solution)/shard_map/dot_general | solution.py:87
  150.0 0.1 fusion.61
  150.1 1.3 collective-permute-start.1
  151.4 6.3 %collective-permute-start = (bf16[3,128,1024]{2,1,0:T(8,128)(2,1)S(1)}, bf16[3,128,1024]{2,1,0:T(8,128)(2,1)S(1)}, u32[]{:S(2)}, u32[]{:S(2)}) collective-permute-start(bf16[3,128,1024]{2,1,0:T(8,128)(2,1)S(1)} %bitcast.128), channel_id=1, source_target_pairs={{0,1},{1,2},{2,3},{3,4},{4,5},{5,6},{6,7},{8,9},{9,10},{10,11},{11... | collective-permute-start | bytes 2359304 | tf_op jit(solution)/shard_map/ppermute | solution.py:41
  157.7 0.0 copy-done.5
  157.8 0.1 fusion.62
  157.9 0.1 fusion.63
  157.9 13.1 %collective-permute-done.1 = bf16[3,128,1024]{2,1,0:T(8,128)(2,1)S(1)} collective-permute-done((bf16[3,128,1024]{2,1,0:T(8,128)(2,1)S(1)}, bf16[3,128,1024]{2,1,0:T(8,128)(2,1)S(1)}, u32[]{:S(2)}, u32[]{:S(2)}) %collective-permute-start.1) | collective-permute-done | bytes 786464 | tf_op jit(solution)/shard_map/ppermute | solution.py:44
  171.0 15.3 %collective-permute-done = bf16[3,128,1024]{2,1,0:T(8,128)(2,1)S(1)} collective-permute-done((bf16[3,128,1024]{2,1,0:T(8,128)(2,1)S(1)}, bf16[3,128,1024]{2,1,0:T(8,128)(2,1)S(1)}, u32[]{:S(2)}, u32[]{:S(2)}) %collective-permute-start) | collective-permute-done | bytes 786464 | tf_op jit(solution)/shard_map/ppermute | solution.py:41
  186.4 2.3 fusion.14
  188.7 37.1 %fusion.60 = (f32[8,128]{1,0:T(8,128)S(1)}, f32[8,128,1024]{2,1,0:T(8,128)S(1)}) fusion(f32[1024]{0:T(1024)S(1)} %bitcast.141, bf16[14,131,1024]{2,1,0:T(8,128)(2,1)S(1)} %get-tuple-element.10, f32[1024]{0:T(1024)S(1)} %bitcast.142, f32[1024]{0:T(1024)S(1)} %bitcast.144, f32[1024]{0:T(1024)S(1)} %bitcast.145, ...), kind=kLoop, calls=%fused_computation.82 | loop fusion | flops 160431104 | bytes 96149504 | tf_op jit(solution)/shard_map/reduce_sum | solution.py:99
  225.8 0.0 copy-start.7
  225.8 0.5 multiply_reduce_fusion
  226.3 0.0 copy-start.8
  226.3 0.0 copy-start.9
  226.4 0.1 copy-done.7
  226.5 0.6 multiply_convert_fusion
  227.0 0.9 copy-done.8
  227.9 0.0 copy-done.9
  227.9 4.8 %fusion.12 = bf16[1024,1024]{1,0:T(8,128)(2,1)} fusion(bf16[1024,1024]{1,0:T(8,128)(2,1)S(1)} %fusion.2, f32[1024]{0:T(1024)S(1)} %copy-done.9, bf16[1024,1024]{1,0:T(8,128)(2,1)S(1)} %bitcast.123, bf16[1024,1024]{1,0:T(8,128)(2,1)S(1)} %copy-done.8), kind=kOutput, calls=%fused_computation.15 | convolution fusion | flops 2160066560 | bytes 8392704 | tf_op jit(solution)/shard_map/dot_general | solution.py:102
  (7 shorter events, 0.1 us)
Async XLA Ops:
  6.5 2.2 copy-start
  6.5 58.2 %reduce-scatter.5.cloned.1.call-start = ((), (), s32[]{:S(2)}) async-start(), calls=%async_computation.6 | async-start | bytes 2621440 | tf_op jit(solution)/shard_map/reduce_scatter | solution.py:22
  12.9 1.9 copy-start.1
  30.2 3.0 %copy-start.3 = (bf16[1,8,128,1024]{3,2,1,0:T(8,128)(2,1)S(1)}, bf16[1,8,128,1024]{3,2,1,0:T(8,128)(2,1)}, u32[]{:S(2)}) copy-start(bf16[1,8,128,1024]{3,2,1,0:T(8,128)(2,1)} %param.10) | copy-start | bytes 6291460
  36.8 50.1 %copy-start.6 = (f32[1024]{0:T(1024)S(1)}, f32[1024]{0:T(1024)}, u32[]{:S(2)}) copy-start(f32[1024]{0:T(1024)} %param.13) | copy-start | bytes 12292
  36.8 48.7 %reduce-scatter.7.cloned.1.call-start = ((), (), s32[]{:S(2)}) async-start(), calls=%async_computation.7 | async-start | bytes 786432
  113.8 33.8 %copy-start.2 = (f32[1024,1024]{0,1:T(8,128)S(1)}, f32[1024,1024]{0,1:T(8,128)}, u32[]{:S(2)}) copy-start(f32[1024,1024]{0,1:T(8,128)} %copy-done.1) | copy-start | bytes 12582916
  113.8 33.8 %copy-start.4 = (bf16[1,8,128,1024]{3,2,1,0:T(8,128)(2,1)S(1)}, bf16[1,8,128,1024]{3,2,1,0:T(8,128)(2,1)}, u32[]{:S(2)}) copy-start(bf16[1,8,128,1024]{3,2,1,0:T(8,128)(2,1)} %param.10) | copy-start | bytes 6291460
  147.6 10.2 %copy-start.5 = (f32[7,7,1024]{2,1,0:T(8,128)S(1)}, f32[7,7,1024]{2,1,0:T(8,128)}, u32[]{:S(2)}) copy-start(f32[7,7,1024]{2,1,0:T(8,128)} %param.16) | copy-start | bytes 602116
  150.1 20.9 %collective-permute-start.1 = (bf16[3,128,1024]{2,1,0:T(8,128)(2,1)S(1)}, bf16[3,128,1024]{2,1,0:T(8,128)(2,1)S(1)}, u32[]{:S(2)}, u32[]{:S(2)}) collective-permute-start(bf16[3,128,1024]{2,1,0:T(8,128)(2,1)S(1)} %bitcast.129), channel_id=1, source_target_pairs={{1,0},{2,1},{3,2},{4,3},{5,4},{6,5},{7,6},{9,8},{10,9},{11,10},{12... | collective-permute-start | bytes 2359304 | tf_op jit(solution)/shard_map/ppermute | solution.py:44
  151.4 34.9 %collective-permute-start = (bf16[3,128,1024]{2,1,0:T(8,128)(2,1)S(1)}, bf16[3,128,1024]{2,1,0:T(8,128)(2,1)S(1)}, u32[]{:S(2)}, u32[]{:S(2)}) collective-permute-start(bf16[3,128,1024]{2,1,0:T(8,128)(2,1)S(1)} %bitcast.128), channel_id=1, source_target_pairs={{0,1},{1,2},{2,3},{3,4},{4,5},{5,6},{6,7},{8,9},{9,10},{10,11},{11... | collective-permute-start | bytes 2359304 | tf_op jit(solution)/shard_map/ppermute | solution.py:41
  225.8 0.7 copy-start.7
  226.3 1.6 copy-start.8
  226.3 1.6 copy-start.9
Sparse Core Ops, SparseCore 0:
  36.9 27.7 reduce-scatter.4
  67.1 18.4 reduce-scatter.6
where the time goes:
time: 241 us; the launch traced here: 240 us
  waiting for transfers between devices  75.3 us (31%)
  blocking collectives  71.1 us (30%)
  other arithmetic  46.9 us (19%)
  matrix products  18.1 us (8%)
  between operations  13.7 us (6%)
  starting transfers between devices  7.62 us (3%)
  local copies, waits for them, and re-layouts  6.93 us (3%)
    all_to_all x2, blocking collectives, from_everyone(): lax.all_to_all(jnp.broadcast_to(x[None], (size, *x.shape)), axis, 0, 0, t...  48.1 us
    reduce_sum x1, other arithmetic, local(): center = conv - jnp.mean(conv, axis=-1, keepdims=True)  37.1 us
    reduce_scatter x1, waiting for transfers between devices, summed_rows(): x = lax.psum_scatter(x, axis, scatter_dimension=dim, tiled=True)  27.9 us
    unnamed x3, waiting for transfers between devices  18.9 us
    ppermute x1, waiting for transfers between devices, with_halo(): lax.ppermute(lax.slice_in_dim(block, block.shape[dim] - width, None, axis...  15.3 us
    ppermute x1, waiting for transfers between devices, with_halo(): lax.ppermute(lax.slice_in_dim(block, 0, width, axis=dim), axis, backward)  13.1 us
    all_to_all x1, blocking collectives, local(): lax.all_to_all(local_in, 'fc', split_axis=0, concat_axis=0, tiled=True)  12.4 us
    all_to_all x1, blocking collectives, local(): lax.all_to_all(expert_out, 'fc', split_axis=0, concat_axis=0, tiled=True)  10.6 us
  transfers between devices with their start and end apart: 4, of which 4 were waited for; matrix products, arithmetic and copies ran while one was open for 0% of the time, Pallas kernels for 0%

commit v1 on v0

--- a/solution.py
+++ b/solution.py
@@ -1,11 +1,108 @@
 import jax
 import jax.numpy as jnp
 from jax import lax
+from jax.experimental import pallas as pl
+from jax.experimental.pallas import tpu as pltpu
 from jax.sharding import Mesh
 from jax.sharding import PartitionSpec as P
 
+BF = jnp.bfloat16
+F32 = jnp.float32
 TOK = ("tok_0", "tok_1")
 FC_TOK = ("fc", "tok_0", "tok_1")
+
+
+def tree_sum(terms):
+    terms = list(terms)
+    while len(terms) > 1:
+        nxt = [terms[i] + terms[i + 1] for i in range(0, len(terms) - 1, 2)]
+        if len(terms) % 2:
+            nxt.append(terms[-1])
+        terms = nxt
+    return terms[0]
+
+
+def block_kernel(
+    state_ref, cw_ref, gain_ref, scale_ref, proj_hbm, out_hbm,
+    wide, taps, conv, outs, proj, proj_sem, out_sem,
+):
+    width = state_ref.shape[2]
+    chunks = width // 128
+    load_proj = pltpu.make_async_copy(proj_hbm, proj, proj_sem)
+    load_proj.start()
+
+    @pl.loop(0, chunks)
+    def _(k):
+        lane = pl.ds(pl.multiple_of(k * 128, 128), 128)
+        for tap in range(49):
+            row = cw_ref[pl.ds(tap, 1), lane]
+            taps[tap] = jnp.broadcast_to(row, (16, 128)).astype(BF)
+
+        @pl.loop(0, 14)
+        def _(r):
+            v = state_ref[r, :, lane].astype(F32)
+            wide[r, pl.ds(8, 128), :] = v
+            wide[r, pl.ds(0, 8), :] = v[120:128]
+            wide[r, pl.ds(136, 8), :] = v[0:8]
+
+        @pl.loop(0, 8)
+        def _(i):
+            acc = [[None] * 4, [None] * 4]
+            for b in range(7):
+                wv = [taps[a * 7 + b] for a in range(7)]
+                for blk in range(2):
+                    start = i * 16 + (8 * blk + 5 + b)
+                    v = [wide[r, pl.ds(start, 8), :] for r in range(14)]
+                    pk = [jnp.concatenate([v[q], v[q + 4]], axis=0).astype(BF) for q in range(10)]
+                    for p in range(4):
+                        t = tree_sum(pk[p + a] * wv[a] for a in range(7))
+                        acc[blk][p] = t if acc[blk][p] is None else acc[blk][p] + t
+            for blk in range(2):
+                for p in range(4):
+                    f = acc[blk][p].astype(F32)
+                    at = pl.multiple_of(i * 16 + 8 * blk, 8)
+                    conv[p, pl.ds(at, 8), lane] = f[0:8]
+                    conv[p + 4, pl.ds(at, 8), lane] = f[8:16]
+
+    load_proj.wait()
+
+    @pl.loop(0, 8)
+    def _(r):
+        c = conv[r]
+        mean = jnp.mean(c, axis=-1, keepdims=True)
+        center = c - mean
+        spread = jnp.mean(center * center, axis=-1, keepdims=True)
+        normal = (center * lax.rsqrt(spread + 1e-06) * gain_ref[...]).astype(BF)
+        branch = jnp.dot(normal, proj[...], preferred_element_type=F32)
+        res = state_ref[r + 3].astype(F32) + scale_ref[...] * jax.nn.gelu(branch)
+        outs[r] = res.astype(BF)
+        pltpu.make_async_copy(outs.at[r], out_hbm.at[r], out_sem.at[r]).start()
+
+    for r in range(8):
+        pltpu.make_async_copy(outs.at[r], out_hbm.at[r], out_sem.at[r]).wait()
+
+
+def block(state14, conv_weight, ln_gain, layer_scale, proj):
+    width = state14.shape[2]
+    vm = pl.BlockSpec(memory_space=pltpu.VMEM)
+    anyspec = pl.BlockSpec(memory_space=pl.ANY)
+    return pl.pallas_call(
+        block_kernel,
+        out_shape=jax.ShapeDtypeStruct((8, 128, width), BF),
+        in_specs=[vm, vm, vm, vm, anyspec],
+        out_specs=anyspec,
+        scratch_shapes=[
+            pltpu.VMEM((14, 144, 128), F32),
+            pltpu.VMEM((49, 16, 128), BF),
+            pltpu.VMEM((8, 128, width), F32),
+            pltpu.VMEM((8, 128, width), BF),
+            pltpu.VMEM((width, width), BF),
+            pltpu.SemaphoreType.DMA,
+            pltpu.SemaphoreType.DMA((8,)),
+        ],
+        compiler_params=pltpu.CompilerParams(vmem_limit_bytes=60 * 1024 * 1024),
+        name="block",
+    )(state14, conv_weight.reshape(49, width), ln_gain.reshape(1, width), layer_scale.reshape(1, width), proj)
 
 
 def from_everyone(x, axis):
@@ -87,23 +184,8 @@
     mixed = jnp.dot(combine, every_slot, preferred_element_type=jnp.float32)
     state = (cells.astype(jnp.float32) + mixed).astype(jnp.bfloat16).reshape(rows, cols, width)
     padded = with_halo(state, ((TOK, 0),), 3)
-    padded = jnp.concatenate([padded[:, cols - 3 :], padded, padded[:, :3]], axis=1)
-    conv = jnp.zeros((rows, cols, width), jnp.float32)
-    for row_tap in range(7):
-        for col_tap in range(7):
-            conv = (
-                conv
-                + padded[row_tap : row_tap + rows, col_tap : col_tap + cols].astype(jnp.float32)
-                * conv_weight[row_tap, col_tap]
-            )
-    center = conv - jnp.mean(conv, axis=-1, keepdims=True)
-    spread = jnp.mean(center * center, axis=-1, keepdims=True)
-    normal = (center * lax.rsqrt(spread + 1e-06) * ln_gain).astype(jnp.bfloat16)
-    branch = jnp.dot(normal.reshape(rows * cols, width), proj, preferred_element_type=jnp.float32)
-    result = state.reshape(rows * cols, width).astype(jnp.float32) + layer_scale * jax.nn.gelu(
-        branch
-    )
-    return result.astype(jnp.bfloat16).reshape(1, rows, cols, width)
+    result = block(padded, conv_weight, ln_gain, layer_scale, proj)
+    return result.reshape(1, rows, cols, width)
 
 
 def solution(mesh):

time: 241 us -> 222 us (0.921)
  other arithmetic: 46.9 us -> 9.76 us
  Pallas kernels: 0 us -> 20.8 us
  matrix products: 18.1 us -> 11.7 us
  local copies, waits for them, and re-layouts: 6.93 us -> 10.8 us
  starting transfers between devices: 7.62 us -> 4.48 us
    reduce_sum x2 -> x0, other arithmetic: 37.6 us -> none  [the longest x1 37.1 us: local(): center = conv - jnp.mean(conv, axis=-1, keepdims=True)]
    pallas_call x0 -> x1, Pallas kernels: none -> 20.8 us  [block(): pl.pallas_call(block_kernel, out_shape=jax.ShapeDtypeStruct((8, 128, widt...]
    ppermute x1, waiting for transfers between devices: 15.3 us -> 30.5 us  [with_halo(): lax.ppermute(lax.slice_in_dim(block, block.shape[dim] - width, None, axis...]
    ppermute x1, waiting for transfers between devices: 13.1 us -> 0.01 us  [with_halo(): lax.ppermute(lax.slice_in_dim(block, 0, width, axis=dim), axis, backward)]
    dot_general x1 -> x0, matrix products: 4.79 us -> none  [local(): jnp.dot(normal.reshape(rows * cols, width), proj, preferred_element_type=...]
    ppermute x1, starting transfers between devices: 6.28 us -> 3.15 us  [with_halo(): lax.ppermute(lax.slice_in_dim(block, block.shape[dim] - width, None, axis...]
  transfers between devices with their start and end apart: 4 -> 4, of which waited for: 4 -> 3; matrix products, arithmetic and copies ran while one was open for 0% -> 0% of each run, Pallas kernels for 0% -> 0%
where the time goes in v1:
time: 222 us; the launch traced here: 219 us
  waiting for transfers between devices  77.3 us (35%)
  blocking collectives  71 us (32%)
  Pallas kernels  20.8 us (9%)
  between operations  13.6 us (6%)
  matrix products  11.7 us (5%)
  local copies, waits for them, and re-layouts  10.8 us (5%)
  other arithmetic  9.76 us (4%)
  starting transfers between devices  4.48 us (2%)
    all_to_all x2, blocking collectives, from_everyone(): lax.all_to_all(jnp.broadcast_to(x[None], (size, *x.shape)), axis, 0, 0, t...  48 us
    ppermute x1, waiting for transfers between devices, with_halo(): lax.ppermute(lax.slice_in_dim(block, block.shape[dim] - width, None, axis...  30.5 us
    reduce_scatter x1, waiting for transfers between devices, summed_rows(): x = lax.psum_scatter(x, axis, scatter_dimension=dim, tiled=True)  27.9 us
    pallas_call x1, Pallas kernels, block(): pl.pallas_call(block_kernel, out_shape=jax.ShapeDtypeStruct((8, 128, widt...  20.8 us
    unnamed x3, waiting for transfers between devices  19 us
    all_to_all x1, blocking collectives, local(): lax.all_to_all(local_in, 'fc', split_axis=0, concat_axis=0, tiled=True)  12.4 us
    all_to_all x1, blocking collectives, local(): lax.all_to_all(expert_out, 'fc', split_axis=0, concat_axis=0, tiled=True)  10.6 us
    unnamed x22, local copies, waits for them, and re-layouts  8.08 us
  transfers between devices with their start and end apart: 4, of which 3 were waited for; matrix products, arithmetic and copies ran while one was open for 0% of the time, Pallas kernels for 0%

profile of v1, /device:TPU:0, one launch (start us, length us, event | category | flops | bytes accessed | tf_op | source)
XLA Modules:
  0.0 219.4 jit_solution(8548653932340382574)
XLA Ops:
  6.5 0.0 copy-start
  6.5 0.0 copy-start.9
  6.5 0.0 reduce-scatter.5.cloned.1.call-start
  6.5 0.0 copy-start.4
  6.5 2.2 %multiply_reduce_fusion = f32[8,128]{1,0:T(8,128)S(1)} fusion(bf16[1,8,128,1024]{3,2,1,0:T(8,128)(2,1)} %param.10), kind=kLoop, calls=%fused_computation.8 | loop fusion | flops 3144704 | bytes 2101248 | tf_op jit(solution)/shard_map/reduce_sum | solution.py:147
  8.8 0.0 copy-done
  8.8 0.0 copy-done.9
  8.8 0.6 copy-done.4
  9.4 2.5 %fusion.45 = (f32[1024]{0:T(1024)S(1)}, f32[1024,1024]{0,1:T(8,128)S(1)}) fusion(bf16[1024,1024]{1,0:T(8,128)(2,1)S(1)} %copy-done, bf16[1024,1024]{1,0:T(8,128)(2,1)S(1)} %bitcast.69, f32[1024]{0:T(1024)S(1)} %copy-done.9, f32[1024]{0:T(1024)S(1)} %rsqrt_bitcast_fusion), kind=kOutput, calls=%fused_computation.48 | convolution fusion | flops 2152725504 | bytes 8400896 | tf_op jit(solution)/shard_map/dot_general | solution.py:162
  11.9 0.0 copy-start.1
  11.9 0.8 fusion.3
  12.7 1.2 copy-done.1
  13.8 14.6 %all_to_all.21 = f32[8,1,1024]{2,1,0:T(1,128)S(1)} all-to-all(f32[8,1,1024]{2,1,0:T(1,128)S(1)} %broadcast_in_dim.4), channel_id=1, replica_groups=mesh['fc'=16,'tok_0'=4,'tok_1'=2] {'tok_0','tok_1'}, dimensions={0} | all-to-all | bytes 65536 | tf_op jit(solution)/shard_map/all_to_all | solution.py:110
  28.4 0.0 copy-start.5
  28.5 2.9 %exponential_convert_fusion = bf16[1024,1024]{0,1:T(8,128)(2,1)S(1)} fusion(f32[1024,1024]{0,1:T(8,128)} %copy-done.1, f32[1024]{0:T(1024)S(1)} %reduce_max.29), kind=kLoop, calls=%fused_computation.5 | loop fusion | flops 2097152 | bytes 6295552 | tf_op jit(solution)/shard_map/convert_element_type | solution.py:165
  31.4 0.0 copy-done.5
  31.4 3.7 %convolution_convert_fusion = bf16[16,64,1024]{2,1,0:T(8,128)(2,1)} fusion(bf16[16,64,1024]{2,1,0:T(8,128)(2,1)S(1)} %bitcast.73, bf16[1024,1024,1]{1,0,2:T(8,128)(2,1)S(1)} %bitcast.70), kind=kOutput, calls=%fused_computation.19 | convolution fusion | flops 2148532224 | bytes 6291456 | tf_op jit(solution)/shard_map/dot_general | solution.py:166
  35.1 0.0 copy-start.8
  35.1 0.0 reduce-scatter.5.cloned.1.call-update
  35.1 0.0 reduce-scatter.7.cloned.1.call-start
  35.2 27.9 %reduce-scatter.5.cloned.1.call-done = bf16[16,16,1024]{2,1,0:T(8,128)(2,1)} async-done(((bf16[16,64,1024]{2,1,0:T(8,128)(2,1)}), bf16[16,16,1024]{2,1,0:T(8,128)(2,1)}) %reduce-scatter.5.cloned.1.call-update) | async-done | bytes 524304 | tf_op jit(solution)/shard_map/reduce_scatter | solution.py:119
  63.0 1.9 copy.30
  64.9 0.0 reduce-scatter.7.cloned.1.call-update
  64.9 18.9 %reduce-scatter.7.cloned.1.call-done = bf16[8,16384]{1,0:T(8,128)(2,1)} async-done(((bf16[16,16384]{1,0:T(8,128)(2,1)}), bf16[8,16384]{1,0:T(8,128)(2,1)}) %reduce-scatter.7.cloned.1.call-update) | async-done | bytes 262160
  83.8 1.1 copy.36
  84.9 0.2 fusion.19
  85.2 0.0 copy-done.8
  85.2 0.2 fusion.21
  85.4 12.4 %all_to_all.22 = bf16[16,8,1024]{2,1,0:T(8,128)(2,1)S(1)} all-to-all(bf16[16,8,1024]{2,1,0:T(8,128)(2,1)S(1)} %fusion.21), channel_id=1, replica_groups=mesh['fc'=16,'tok_0'=4,'tok_1'=2] {'fc'}, dimensions={0} | all-to-all | bytes 524288 | tf_op jit(solution)/shard_map/all_to_all | solution.py:172
  97.7 0.1 copy.22
  97.9 3.1 %fusion.13 = bf16[2,16,4,1024]{3,1,2,0:T(8,128)(2,1)S(1)} fusion(bf16[2,512,1024]{2,1,0:T(8,128)(2,1)} %param.15, bf16[16,2,4,1024]{3,0,2,1:T(8,128)(2,1)S(1)} %bitcast.74, bf16[2,1024,512]{2,1,0:T(8,128)(2,1)} %param.14), kind=kOutput, calls=%fused_computation.20 | convolution fusion | flops 269156352 | bytes 4718592 | tf_op jit(solution)/shard_map/mesf,efd->mesd/dot_general | solution.py:177
  101.0 0.2 copy.23
  101.2 10.6 %all_to_all.23 = bf16[16,8,1024]{2,1,0:T(8,128)(2,1)S(1)} all-to-all(bf16[16,8,1024]{2,1,0:T(8,128)(2,1)S(1)} %copy.23), channel_id=1, replica_groups=mesh['fc'=16,'tok_0'=4,'tok_1'=2] {'fc'}, dimensions={0} | all-to-all | bytes 524288 | tf_op jit(solution)/shard_map/all_to_all | solution.py:181
  111.8 0.3 broadcast_in_dim.5
  112.0 0.0 copy-start.6
  112.0 33.4 %all_to_all.24 = bf16[8,16,8,1024]{3,2,1,0:T(8,128)(2,1)S(1)} all-to-all(bf16[8,16,8,1024]{3,2,1,0:T(8,128)(2,1)S(1)} %broadcast_in_dim.5), channel_id=1, replica_groups=mesh['fc'=16,'tok_0'=4,'tok_1'=2] {'tok_0','tok_1'}, dimensions={0} | all-to-all | bytes 4194304 | tf_op jit(solution)/shard_map/all_to_all | solution.py:110
  145.5 0.0 copy-start.2
  145.5 0.2 copy.24
  145.7 0.0 copy-done.6
  145.7 2.0 copy-done.2
  147.7 2.4 %fusion.2 = bf16[1024,1024]{1,0:T(8,128)(2,1)S(1)} fusion(bf16[1,8,128,1024]{3,2,1,0:T(8,128)(2,1)S(1)} %copy-done.6, bf16[1024,1024]{1,0:T(8,128)(2,1)S(1)} %bitcast.71, f32[1024,1024]{0,1:T(8,128)S(1)} %copy-done.2, f32[1024]{0:T(1024)S(1)} %get-tuple-element.5, f32[1024]{0:T(1024)S(1)} %get-tuple-element.9), kind=kOutput, calls=%fused_computation.4 | convolution fusion | flops 2153775104 | bytes 10493952 | tf_op jit(solution)/shard_map/dot_general | solution.py:184
  150.1 0.0 copy-start.3
  150.1 1.3 copy-done.3
  151.4 0.0 copy-start.7
  151.4 1.3 fusion.44
  152.7 3.1 %collective-permute-start = (bf16[3,128,1024]{2,1,0:T(8,128)(2,1)}, bf16[3,128,1024]{2,1,0:T(8,128)(2,1)S(1)}, u32[]{:S(2)}, u32[]{:S(2)}) collective-permute-start(bf16[3,128,1024]{2,1,0:T(8,128)(2,1)} %bitcast.15), channel_id=1, source_target_pairs={{0,1},{1,2},{2,3},{3,4},{4,5},{5,6},{6,7},{8,9},{9,10},{10,11},{11... | collective-permute-start | bytes 2359304 | tf_op jit(solution)/shard_map/ppermute | solution.py:138
  155.9 1.3 collective-permute-start.1
  157.2 0.0 copy-done.7
  157.2 0.7 reshape.69.cw_ref
  157.9 30.5 %collective-permute-done = bf16[3,128,1024]{2,1,0:T(8,128)(2,1)S(1)} collective-permute-done((bf16[3,128,1024]{2,1,0:T(8,128)(2,1)}, bf16[3,128,1024]{2,1,0:T(8,128)(2,1)S(1)}, u32[]{:S(2)}, u32[]{:S(2)}) %collective-permute-start) | collective-permute-done | bytes 786464 | tf_op jit(solution)/shard_map/ppermute | solution.py:138
  188.4 0.0 collective-permute-done.1
  188.4 3.4 %pad_maximum_fusion.state_ref = bf16[14,128,1024]{2,1,0:T(8,128)(2,1)} fusion(bf16[3,128,1024]{2,1,0:T(8,128)(2,1)} %collective-permute-done.1, bf16[8,128,1024]{2,1,0:T(8,128)(2,1)} %bitcast.66, bf16[3,128,1024]{2,1,0:T(8,128)(2,1)S(1)} %collective-permute-done), kind=kLoop, calls=%fused_computation.10 | loop fusion | flops 3670016 | bytes 7340032 | tf_op jit(solution)/shard_map/concatenate | solution.py:142
  191.8 20.8 %block.1 = bf16[8,128,1024]{2,1,0:T(8,128)(2,1)} custom-call(bf16[14,128,1024]{2,1,0:T(8,128)(2,1)} %pad_maximum_fusion.state_ref, f32[49,1024]{1,0:T(8,128)} %reshape.69.cw_ref, f32[1,1024]{1,0:T(1,128)} %bitcast.78, f32[1,1024]{1,0:T(1,128)} %bitcast.79, bf16[1024,1024]{1,0:T(8,128)(2,1)} %proj_hbm.1), custom_call_target="tpu_custom_call" | custom-call | tf_op jit(solution)/shard_map/block/pallas_call | solution.py:89
  (4 shorter events, 0.1 us)
Async XLA Ops:
  6.5 2.2 %copy-start = (bf16[1024,1024]{1,0:T(8,128)(2,1)S(1)}, bf16[1024,1024]{1,0:T(8,128)(2,1)}, u32[]{:S(2)}) copy-start(bf16[1024,1024]{1,0:T(8,128)(2,1)} %param.11) | copy-start | bytes 6291460
  6.5 2.3 %copy-start.9 = (f32[1024]{0:T(1024)S(1)}, f32[1024]{0:T(1024)}, u32[]{:S(2)}) copy-start(f32[1024]{0:T(1024)} %param.12) | copy-start | bytes 12292
  6.5 56.5 %reduce-scatter.5.cloned.1.call-start = ((), (), s32[]{:S(2)}) async-start(), calls=%async_computation.6 | async-start | bytes 2621440 | tf_op jit(solution)/shard_map/reduce_scatter | solution.py:119
  6.5 2.9 %copy-start.4 = (bf16[1,8,128,1024]{3,2,1,0:T(8,128)(2,1)S(1)}, bf16[1,8,128,1024]{3,2,1,0:T(8,128)(2,1)}, u32[]{:S(2)}) copy-start(bf16[1,8,128,1024]{3,2,1,0:T(8,128)(2,1)} %param.10) | copy-start | bytes 6291460
  11.9 1.9 copy-start.1
  28.4 3.0 %copy-start.5 = (bf16[1,8,128,1024]{3,2,1,0:T(8,128)(2,1)S(1)}, bf16[1,8,128,1024]{3,2,1,0:T(8,128)(2,1)}, u32[]{:S(2)}) copy-start(bf16[1,8,128,1024]{3,2,1,0:T(8,128)(2,1)} %param.10) | copy-start | bytes 6291460
  35.1 50.1 %copy-start.8 = (f32[1024]{0:T(1024)S(1)}, f32[1024]{0:T(1024)}, u32[]{:S(2)}) copy-start(f32[1024]{0:T(1024)} %param.13) | copy-start | bytes 12292
  35.1 48.7 %reduce-scatter.7.cloned.1.call-start = ((), (), s32[]{:S(2)}) async-start(), calls=%async_computation.7 | async-start | bytes 786432
  112.0 33.6 %copy-start.6 = (bf16[1,8,128,1024]{3,2,1,0:T(8,128)(2,1)S(1)}, bf16[1,8,128,1024]{3,2,1,0:T(8,128)(2,1)}, u32[]{:S(2)}) copy-start(bf16[1,8,128,1024]{3,2,1,0:T(8,128)(2,1)} %param.10) | copy-start | bytes 6291460
  145.5 2.2 copy-start.2
  150.1 1.3 copy-start.3
  151.4 5.7 %copy-start.7 = (f32[7,7,1024]{2,1,0:T(8,128)S(1)}, f32[7,7,1024]{2,1,0:T(8,128)}, u32[]{:S(2)}) copy-start(f32[7,7,1024]{2,1,0:T(8,128)} %param.16) | copy-start | bytes 602116
  152.7 35.6 %collective-permute-start = (bf16[3,128,1024]{2,1,0:T(8,128)(2,1)}, bf16[3,128,1024]{2,1,0:T(8,128)(2,1)S(1)}, u32[]{:S(2)}, u32[]{:S(2)}) collective-permute-start(bf16[3,128,1024]{2,1,0:T(8,128)(2,1)} %bitcast.15), channel_id=1, source_target_pairs={{0,1},{1,2},{2,3},{3,4},{4,5},{5,6},{6,7},{8,9},{9,10},{10,11},{11... | collective-permute-start | bytes 2359304 | tf_op jit(solution)/shard_map/ppermute | solution.py:138
  155.9 32.5 %collective-permute-start.1 = (bf16[3,128,1024]{2,1,0:T(8,128)(2,1)}, bf16[3,128,1024]{2,1,0:T(8,128)(2,1)}, u32[]{:S(2)}, u32[]{:S(2)}) collective-permute-start(bf16[3,128,1024]{2,1,0:T(8,128)(2,1)} %bitcast.17), channel_id=1, source_target_pairs={{1,0},{2,1},{3,2},{4,3},{5,4},{6,5},{7,6},{9,8},{10,9},{11,10},{12... | collective-permute-start | bytes 2359304 | tf_op jit(solution)/shard_map/ppermute | solution.py:141
Sparse Core Ops, SparseCore 0:
  35.2 27.7 reduce-scatter.4
  65.4 18.4 reduce-scatter.6

commit v2 on v1

v2 whole, which is shorter than its diff:
```python
import jax
import jax.numpy as jnp
from jax import lax
from jax.experimental import pallas as pl
from jax.experimental.pallas import tpu as pltpu
from jax.sharding import PartitionSpec as P

BF = jnp.bfloat16
F32 = jnp.float32
MESH = pl.DeviceIdType.MESH
MEMBERS_AX = 16
NCH = 4


def rms_scale(value, gain):
    return value * lax.rsqrt(jnp.mean(value * value, axis=-1, keepdims=True) + 1e-06) * gain


def fold_halves(v):
    half = v.shape[-1] // 2
    return jnp.concatenate([v[..., :half], v[..., half:]], axis=-2)


def unfold_halves(v):
    rows = v.shape[-2] // 2
    return jnp.concatenate([v[..., :rows, :], v[..., rows:, :]], axis=-1)


def mix_kernel(
    tok_hbm, keys_hbm, ngain_ref, sgain_ref, win_hbm, wout_hbm, state_hbm,
    cells, keys, win, wout, logits, combine, disp, numer, rx, ysend, yrecv, keep,
    asend, arecv, bsend, brecv, part, every, state, peaks, load_sem,
    peak_ss, peak_rs, halo_ss, halo_rs, x_ss, x_rs, y_ss, y_rs, a_ss, a_rs, b_ss, b_rs,
    p_ss, p_rs, g_ss, g_rs, out_sem,
):
    nf, nt = MEMBERS_AX, 8
    width = cells.shape[2]
    cw = width // NCH
    f = lax.axis_index("fc")
    t = lax.axis_index("tok")
    x = lax.div(t, 2)
    h = lax.rem(t, 2)

    loads = [
        pltpu.make_async_copy(tok_hbm, cells.at[pl.ds(3, 8)], load_sem.at[0]),
        pltpu.make_async_copy(keys_hbm, keys, load_sem.at[1]),
        pltpu.make_async_copy(win_hbm, win, load_sem.at[2]),
        pltpu.make_async_copy(wout_hbm, wout, load_sem.at[3]),
    ]
    for c in loads:
        c.start()

    def at_tok(k):
        return {"fc": f, "tok": k}

    def at_fc(k):
        return {"fc": k, "tok": t}

    barrier = pltpu.get_barrier_semaphore()
    for d in range(1, nt):
        pl.semaphore_signal(barrier, inc=1, device_id=at_tok(lax.rem(t + d, nt)), device_id_type=MESH)
    for d in range(1, nf):
        pl.semaphore_signal(barrier, inc=1, device_id=at_fc(lax.rem(f + d, nf)), device_id_type=MESH)

    def remote(src, dst, ss, rs, dev):
        return pltpu.make_async_remote_copy(
            src_ref=src, dst_ref=dst, send_sem=ss, recv_sem=rs, device_id=dev, device_id_type=MESH
        )

    loads[0].wait()
    loads[1].wait()

    def logits_of(v):
        normed = rms_scale(v.astype(F32), ngain_ref[...]).astype(BF)
        return jnp.dot(normed, keys[...], preferred_element_type=F32)

    def softmax_of(l):
        e = jnp.exp(l - jnp.max(l, axis=-1, keepdims=True))
        return (e / jnp.sum(e, axis=-1, keepdims=True)).astype(BF)

    def first(r, peak):
        v = cells[pl.ds(3 + 2 * r, 2)].reshape(256, width)
        l = logits_of(v)
        logits[pl.ds(2 * r, 2)] = l.reshape(2, 128, width)
        return jnp.maximum(peak, jnp.max(l.reshape(32, 8, width), axis=0))

    peak = lax.fori_loop(0, 4, first, jnp.full((8, width), -jnp.inf, F32))
    peaks[t] = jnp.max(peak, axis=0, keepdims=True)

    pl.semaphore_wait(barrier, nt + nf - 2)
    peak_copies = []
    for d in range(1, nt):
        k = lax.rem(t + d, nt)
        c = remote(peaks.at[t], peaks.at[t], peak_ss.at[d - 1], peak_rs.at[d - 1], at_tok(k))
        c.start()
        peak_copies.append(c)

    def halo_copies(part_at):
        low = remote(
            cells.at[8 + part_at], cells.at[part_at], halo_ss.at[0, part_at], halo_rs.at[0, part_at], at_tok(t + 1)
        )
        high = remote(
            cells.at[3 + part_at], cells.at[11 + part_at], halo_ss.at[1, part_at], halo_rs.at[1, part_at], at_tok(t - 1)
        )
        return low, high

    def start_halo(part_at):
        low, high = halo_copies(part_at)

        @pl.when(t < nt - 1)
        def _():
            low.start()

        @pl.when(t > 0)
        def _():
            high.start()

    start_halo(0)

    @pl.when(t == 0)
    def _():
        cells[pl.ds(0, 3)] = jnp.zeros((3, 128, width), BF)

    @pl.when(t == nt - 1)
    def _():
        cells[pl.ds(11, 3)] = jnp.zeros((3, 128, width), BF)

    @pl.loop(0, 8)
    def _(r):
        combine[3 + r] = softmax_of(logits[r])

    for c in peak_copies:
        c.wait_recv()
    top = peaks[0]
    for k in range(1, nt):
        top = jnp.maximum(top, peaks[k])

    @pl.loop(0, 8)
    def _(r):
        shifted = jnp.exp(logits[r] - top)
        disp[:, pl.ds(pl.multiple_of(r * 128, 128), 128)] = shifted.T.astype(BF)

    x_copies = []
    for n in range(NCH):
        lane = pl.ds(n * cw, cw)
        own = cells[pl.ds(3, 8), :, lane].reshape(1024, cw)
        numer[:, :, :, lane] = (
            jnp.dot(disp[...], own, preferred_element_type=F32).astype(BF).reshape(nf, 4, 16, cw)
        )
        row = []
        for d in range(1, 4):
            k = lax.rem(x + d, 4)
            c = remote(
                numer.at[:, k, :, lane], rx.at[d - 1, :, :, lane], x_ss.at[n, d - 1], x_rs.at[n, d - 1],
                at_tok(k * 2 + h),
            )
            c.start()
            row.append(c)
        x_copies.append(row)

    y_copies = []
    for n in range(NCH):
        lane = pl.ds(n * cw, cw)
        for c in x_copies[n]:
            c.wait_recv()
        total = numer[:, x, :, lane].astype(F32)
        for d in range(3):
            total = total + rx[d, :, :, lane].astype(F32)
        low = total[:, 0:8].reshape(nf * 8, cw)
        high = total[:, 8:16].reshape(nf * 8, cw)
        ysend[:, lane] = jnp.where(h == 0, high, low).astype(BF)
        keep[:, lane] = jnp.where(h == 0, low, high)
        c = remote(
            ysend.at[:, lane], yrecv.at[:, lane], y_ss.at[n], y_rs.at[n], at_tok(x * 2 + 1 - h)
        )
        c.start()
        y_copies.append(c)
        if n == 1:
            start_halo(1)

    for c in y_copies:
        c.wait_recv()
    local_in = rms_scale(keep[...] + yrecv[...].astype(F32), sgain_ref[...])
    asend[...] = fold_halves(local_in.reshape(nf, 8, width)).astype(BF)
    arecv[f] = asend[f]
    a_copies = []
    for d in range(1, nf):
        k = lax.rem(f + d, nf)
        c = remote(asend.at[k], arecv.at[f], a_ss.at[d - 1], a_rs.at[d - 1], at_fc(k))
        c.start()
        a_copies.append(c)
    loads[2].wait()
    loads[3].wait()
    for c in a_copies:
        c.wait_recv()

    lhs = unfold_halves(arecv[...].astype(F32)).reshape(nf * 8, width).astype(BF)
    which = lax.rem(lax.broadcasted_iota(jnp.int32, (nf * 8, 1), 0), 8) < 4
    hid = jnp.where(
        which,
        jnp.dot(lhs, win[0], preferred_element_type=F32),
        jnp.dot(lhs, win[1], preferred_element_type=F32),
    )
    hid = jax.nn.gelu(hid).astype(BF)
    out = jnp.where(
        which,
        jnp.dot(hid, wout[0], preferred_element_type=F32),
        jnp.dot(hid, wout[1], preferred_element_type=F32),
    )
    bsend[...] = fold_halves(out.reshape(nf, 8, width)).astype(BF)
    brecv[f] = bsend[f]
    b_copies = []
    for d in range(1, nf):
        k = lax.rem(f + d, nf)
        c = remote(bsend.at[k], brecv.at[f], b_ss.at[d - 1], b_rs.at[d - 1], at_fc(k))
        c.start()
        b_copies.append(c)
    for c in b_copies:
        c.wait_recv()

    pair = remote(brecv, part, p_ss, p_rs, at_tok(x * 2 + 1 - h))
    pair.start()
    start_halo(2)
    pair.wait_recv()
    mine = unfold_halves(brecv[...].astype(F32))
    theirs = unfold_halves(part[...].astype(F32))
    low = jnp.where(h == 0, mine, theirs)
    high = jnp.where(h == 0, theirs, mine)
    every[:, x] = jnp.concatenate([low, high], axis=1).astype(BF)

    g_copies = []
    for n in range(NCH):
        lane = pl.ds(n * cw, cw)
        row = []
        for d in range(1, 4):
            k = lax.rem(x + d, 4)
            c = remote(
                every.at[:, x, :, lane], every.at[:, x, :, lane], g_ss.at[n, d - 1], g_rs.at[n, d - 1],
                at_tok(k * 2 + h),
            )
            c.start()
            row.append(c)
        g_copies.append(row)

    for p in range(3):
        lo_copy, hi_copy = halo_copies(p)

        @pl.when(t > 0)
        def _():
            lo_copy.wait_recv()

        @pl.when(t < nt - 1)
        def _():
            hi_copy.wait_recv()

    @pl.loop(0, 6)
    def _(i):
        r = i + 8 * lax.div(i, 3)
        combine[r] = softmax_of(logits_of(cells[r]))

    outs = []
    rows = 7 * 128
    for n in range(NCH):
        lane = pl.ds(n * cw, cw)
        for c in g_copies[n]:
            c.wait_recv()
        rhs = every[:, :, :, lane].reshape(1024, cw)

        @pl.loop(0, 2)
        def _(b):
            mixed = jnp.dot(
                combine[pl.ds(b * 7, 7)].reshape(rows, width), rhs, preferred_element_type=F32
            )
            v = cells[pl.ds(b * 7, 7), :, lane].reshape(rows, cw).astype(F32) + mixed
            at = lax.broadcasted_iota(jnp.int32, (rows, 1), 0) + (b * rows + (8 * t - 3) * 128)
            inside = jnp.logical_and(at >= 0, at < 64 * 128)
            v = jnp.where(inside, v, 0.0)
            state[pl.ds(b * 7, 7), :, lane] = v.astype(BF).reshape(7, 128, cw)

        o = pltpu.make_async_copy(state.at[:, :, lane], state_hbm.at[:, :, lane], out_sem.at[n])
        o.start()
        outs.append(o)

    for c in peak_copies + [c for row in x_copies for c in row] + y_copies + a_copies + b_copies:
        c.wait_send()
    pair.wait_send()
    for row in g_copies:
        for c in row:
            c.wait_send()
    for p in range(3):
        lo_copy, hi_copy = halo_copies(p)

        @pl.when(t < nt - 1)
        def _():
            lo_copy.wait_send()

        @pl.when(t > 0)
        def _():
            hi_copy.wait_send()

    for o in outs:
        o.wait()


def mixed_state(tokens, slot_keys, norm_gain, slot_gain, w_in, w_out):
    width = tokens.shape[2]
    vm = pl.BlockSpec(memory_space=pltpu.VMEM)
    anyspec = pl.BlockSpec(memory_space=pl.ANY)
    dma = pltpu.SemaphoreType.DMA
    nf = MEMBERS_AX
    return pl.pallas_call(
        mix_kernel,
        out_shape=jax.ShapeDtypeStruct((14, 128, width), BF),
        in_specs=[anyspec, anyspec, vm, vm, anyspec, anyspec],
        out_specs=anyspec,
        scratch_shapes=[
            pltpu.VMEM((14, 128, width), BF),
            pltpu.VMEM((width, width), BF),
            pltpu.VMEM(w_in.shape, BF),
            pltpu.VMEM(w_out.shape, BF),
            pltpu.VMEM((8, 128, width), F32),
            pltpu.VMEM((14, 128, width), BF),
            pltpu.VMEM((width, 1024), BF),
            pltpu.VMEM((nf, 4, 16, width), BF),
            pltpu.VMEM((3, nf, 16, width), BF),
            pltpu.VMEM((nf * 8, width), BF),
            pltpu.VMEM((nf * 8, width), BF),
            pltpu.VMEM((nf * 8, width), F32),
            pltpu.VMEM((nf, 16, width // 2), BF),
            pltpu.VMEM((nf, 16, width // 2), BF),
            pltpu.VMEM((nf, 16, width // 2), BF),
            pltpu.VMEM((nf, 16, width // 2), BF),
            pltpu.VMEM((nf, 16, width // 2), BF),
            pltpu.VMEM((nf, 4, 16, width), BF),
            pltpu.VMEM((14, 128, width), BF),
            pltpu.VMEM((8, 1, width), F32),
            dma((4,)),
            dma((7,)), dma((7,)),
            dma((2, 3)), dma((2, 3)),
            dma((NCH, 3)), dma((NCH, 3)),
            dma((NCH,)), dma((NCH,)),
            dma((15,)), dma((15,)),
            dma((15,)), dma((15,)),
            dma, dma,
            dma((NCH, 3)), dma((NCH, 3)),
            dma((NCH,)),
        ],
        compiler_params=pltpu.CompilerParams(
            collective_id=0, has_side_effects=True, vmem_limit_bytes=62 * 1024 * 1024
        ),
        name="mix",
    )(tokens, slot_keys, norm_gain.reshape(1, width), slot_gain.reshape(1, width), w_in, w_out)


def tree_sum(terms):
    terms = list(terms)
    while len(terms) > 1:
        nxt = [terms[i] + terms[i + 1] for i in range(0, len(terms) - 1, 2)]
        if len(terms) % 2:
            nxt.append(terms[-1])
        terms = nxt
    return terms[0]


def block_kernel(
    state_ref, cw_ref, gain_ref, scale_ref, proj_hbm, out_hbm,
    wide, taps, conv, outs, proj, proj_sem, out_sem,
):
    width = state_ref.shape[2]
    chunks = width // 128
    load_proj = pltpu.make_async_copy(proj_hbm, proj, proj_sem)
    load_proj.start()

    @pl.loop(0, chunks)
    def _(k):
        lane = pl.ds(pl.multiple_of(k * 128, 128), 128)
        for tap in range(49):
            row = cw_ref[pl.ds(tap, 1), lane]
            taps[tap] = jnp.broadcast_to(row, (16, 128)).astype(BF)

        @pl.loop(0, 14)
        def _(r):
            v = state_ref[r, :, lane].astype(F32)
            wide[r, pl.ds(8, 128), :] = v
            wide[r, pl.ds(0, 8), :] = v[120:128]
            wide[r, pl.ds(136, 8), :] = v[0:8]

        @pl.loop(0, 8)
        def _(i):
            acc = [[None] * 4, [None] * 4]
            for b in range(7):
                wv = [taps[a * 7 + b] for a in range(7)]
                for blk in range(2):
                    start = i * 16 + (8 * blk + 5 + b)
                    v = [wide[r, pl.ds(start, 8), :] for r in range(14)]
                    pk = [jnp.concatenate([v[q], v[q + 4]], axis=0).astype(BF) for q in range(10)]
                    for p in range(4):
                        t = tree_sum(pk[p + a] * wv[a] for a in range(7))
                        acc[blk][p] = t if acc[blk][p] is None else acc[blk][p] + t
            for blk in range(2):
                for p in range(4):
                    f = acc[blk][p].astype(F32)
                    at = pl.multiple_of(i * 16 + 8 * blk, 8)
                    conv[p, pl.ds(at, 8), lane] = f[0:8]
                    conv[p + 4, pl.ds(at, 8), lane] = f[8:16]

    load_proj.wait()

    @pl.loop(0, 8)
    def _(r):
        c = conv[r]
        mean = jnp.mean(c, axis=-1, keepdims=True)
        center = c - mean
        spread = jnp.mean(center * center, axis=-1, keepdims=True)
        normal = (center * lax.rsqrt(spread + 1e-06) * gain_ref[...]).astype(BF)
        branch = jnp.dot(normal, proj[...], preferred_element_type=F32)
        res = state_ref[r + 3].astype(F32) + scale_ref[...] * jax.nn.gelu(branch)
        outs[r] = res.astype(BF)
        pltpu.make_async_copy(outs.at[r], out_hbm.at[r], out_sem.at[r]).start()

    for r in range(8):
        pltpu.make_async_copy(outs.at[r], out_hbm.at[r], out_sem.at[r]).wait()


def block(state14, conv_weight, ln_gain, layer_scale, proj):
    width = state14.shape[2]
    vm = pl.BlockSpec(memory_space=pltpu.VMEM)
    anyspec = pl.BlockSpec(memory_space=pl.ANY)
    return pl.pallas_call(
        block_kernel,
        out_shape=jax.ShapeDtypeStruct((8, 128, width), BF),
        in_specs=[vm, vm, vm, vm, anyspec],
        out_specs=anyspec,
        scratch_shapes=[
            pltpu.VMEM((14, 144, 128), F32),
            pltpu.VMEM((49, 16, 128), BF),
            pltpu.VMEM((8, 128, width), F32),
            pltpu.VMEM((8, 128, width), BF),
            pltpu.VMEM((width, width), BF),
            pltpu.SemaphoreType.DMA,
            pltpu.SemaphoreType.DMA((8,)),
        ],
        compiler_params=pltpu.CompilerParams(vmem_limit_bytes=60 * 1024 * 1024),
        name="block",
    )(state14, conv_weight.reshape(49, width), ln_gain.reshape(1, width), layer_scale.reshape(1, width), proj)


def local(
    tokens, slot_keys, norm_gain, slot_gain, w_in, w_out, conv_weight, ln_gain, proj, layer_scale
):
    state = mixed_state(tokens[0], slot_keys, norm_gain, slot_gain, w_in, w_out)
    return block(state, conv_weight, ln_gain, layer_scale, proj)[None]


def solution(mesh):
    in_specs = (
        P("fc", "tok", None, None),
        P(),
        P(),
        P(),
        P(("fc", "tok"), None, None),
        P(("fc", "tok"), None, None),
        P(),
        P(),
        P(),
        P(),
    )
    out_specs = P("fc", "tok", None, None)
    return jax.shard_map(local, mesh=mesh, in_specs=in_specs, out_specs=out_specs, check_vma=False)
```

time: 222 us -> 127 us (0.57)
  Pallas kernels: 20.8 us -> 125 us
  waiting for transfers between devices: 77.3 us -> 0 us
  blocking collectives: 71 us -> 0 us
  between operations: 13.6 us -> 0.01 us
  matrix products: 11.7 us -> 0 us
  other arithmetic: 9.76 us -> 0 us
  local copies, waits for them, and re-layouts: 10.8 us -> 1.66 us
  starting transfers between devices: 4.48 us -> 0 us
    pallas_call x0 -> x1, Pallas kernels: none -> 104 us  [mixed_state(): pl.pallas_call(mix_kernel, out_shape=jax.ShapeDtypeStruct((14, 128, width...]
    all_to_all x4 -> x0, blocking collectives: 71 us -> none  [the longest x2 48 us: from_everyone(): lax.all_to_all(jnp.broadcast_to(x[None], (size, *x.shape)), axis, 0, 0, t...]
    ppermute x2 -> x0, waiting for transfers between devices: 30.5 us -> none  [the longest x1 30.5 us: with_halo(): lax.ppermute(lax.slice_in_dim(block, block.shape[dim] - width, None, axis...]
    reduce_scatter x1 -> x0, waiting for transfers between devices: 27.9 us -> none  [summed_rows(): x = lax.psum_scatter(x, axis, scatter_dimension=dim, tiled=True)]
    unnamed x3 -> x0, waiting for transfers between devices: 19 us -> none
    dot_general x4 -> x0, matrix products: 11.7 us -> none  [the longest x1 3.65 us: local(): lax.dot_general(dispatch, cells, (((0,), (0,)), ((), ())), preferred_elem...]
    unnamed x22 -> x0, local copies, waits for them, and re-layouts: 8.08 us -> none
    ppermute x2 -> x0, starting transfers between devices: 4.44 us -> none  [the longest x1 3.15 us: with_halo(): lax.ppermute(lax.slice_in_dim(block, block.shape[dim] - width, None, axis...]
  transfers between devices with their start and end apart: 4 -> 0, of which waited for: 3 -> 0; matrix products, arithmetic and copies ran while one was open for 0% -> 0% of each run, Pallas kernels for 0% -> 0%
where the time goes in v2:
time: 127 us; the launch traced here: 126 us
  Pallas kernels  125 us (98%)
  local copies, waits for them, and re-layouts  1.66 us (1%)
    pallas_call x1, Pallas kernels, mixed_state(): pl.pallas_call(mix_kernel, out_shape=jax.ShapeDtypeStruct((14, 128, width...  104 us
    pallas_call x1, Pallas kernels, block(): pl.pallas_call(block_kernel, out_shape=jax.ShapeDtypeStruct((8, 128, widt...  20.8 us

profile of v2, /device:TPU:0, one launch (start us, length us, event | category | flops | bytes accessed | tf_op | source)
XLA Modules:
  0.0 126.4 jit_solution(5363989610566765634)
XLA Ops:
  0.0 1.7 %reshape.17.cw_ref = f32[49,1024]{1,0:T(8,128)} reshape(f32[7,7,1024]{2,1,0:T(8,128)} %param.16) | data formatting | bytes 401408 | tf_op jit(solution)/shard_map/reshape | solution.py:445
  1.7 103.9 %mix.1.state_ref = bf16[14,128,1024]{2,1,0:T(8,128)(2,1)} custom-call(bf16[8,128,1024]{2,1,0:T(8,128)(2,1)} %bitcast.6, bf16[1024,1024]{1,0:T(8,128)(2,1)} %keys_hbm.1, f32[1,1024]{1,0:T(1,128)} %bitcast.7, f32[1,1024]{1,0:T(1,128)} %bitcast.8, bf16[2,1024,512]{2,1,0:T(8,128)(2,1)} %win_hbm.1, bf16[2,512,1024]{2,1,0:T(8,128)(2,1)} %wout_hbm.1), custom_call_target="tpu_custom_call" | custom-call | tf_op jit(solution)/shard_map/mix/pallas_call | solution.py:311
  105.6 20.8 %block.1 = bf16[8,128,1024]{2,1,0:T(8,128)(2,1)} custom-call(bf16[14,128,1024]{2,1,0:T(8,128)(2,1)} %mix.1.state_ref, f32[49,1024]{1,0:T(8,128)} %reshape.17.cw_ref, f32[1,1024]{1,0:T(1,128)} %bitcast.9, f32[1,1024]{1,0:T(1,128)} %bitcast.10, bf16[1024,1024]{1,0:T(8,128)(2,1)} %proj_hbm.1), custom_call_target="tpu_custom_call" | custom-call | tf_op jit(solution)/shard_map/block/pallas_call | solution.py:429

commit v3 on v2

v3 whole, which is shorter than its diff:
```python
import jax
import jax.numpy as jnp
from jax import lax
from jax.experimental import pallas as pl
from jax.experimental.pallas import tpu as pltpu
from jax.sharding import PartitionSpec as P

BF = jnp.bfloat16
F32 = jnp.float32
MESH = pl.DeviceIdType.MESH
MEMBERS_AX = 16
NCH = 4
AT_SEND, AT_RETURN, LATE = (0,), (1,), (2,)


def rms_scale(value, gain):
    return value * lax.rsqrt(jnp.mean(value * value, axis=-1, keepdims=True) + 1e-06) * gain


def fold_halves(v):
    half = v.shape[-1] // 2
    return jnp.concatenate([v[..., :half], v[..., half:]], axis=-2)


def unfold_halves(v):
    rows = v.shape[-2] // 2
    return jnp.concatenate([v[..., :rows, :], v[..., rows:, :]], axis=-1)


def mix_kernel(
    tok_hbm, keys_hbm, ngain_ref, sgain_ref, win_hbm, wout_hbm, cw_ref, lgain_ref, scale_ref, proj_hbm,
    out_hbm,
    cells, keys, win, wout, logits, combine, disp, numer, passed, rx, ysend, yrecv, keep,
    asend, arecv, bsend, every, joined, state, wide, taps, conv, even, odd, outs, proj, peaks, tops, shrink, load_sem,
    peak_ss, peak_rs, top_ss, top_rs, halo_ss, halo_rs, w_ss, w_rs, x_ss, x_rs, y_ss, y_rs, a_ss, a_rs, b_ss, b_rs,
    p_ss, p_rs, g_ss, g_rs, o_ss, o_rs, out_sem,
):
    nf, nt = MEMBERS_AX, 8
    width = cells.shape[2]
    cw = width // NCH
    f = lax.axis_index("fc")
    t = lax.axis_index("tok")
    x = lax.div(t, 2)
    h = lax.rem(t, 2)

    def at_tok(k):
        return {"fc": f, "tok": k}

    def at_fc(k):
        return {"fc": k, "tok": t}

    right, left, across = lax.rem(x + 1, 4), lax.rem(x + 3, 4), lax.rem(x + 2, 4)
    to_right, to_left, to_pair = at_tok(right * 2 + h), at_tok(left * 2 + h), at_tok(x * 2 + 1 - h)

    loads = [
        pltpu.make_async_copy(tok_hbm, cells.at[pl.ds(3, 8)], load_sem.at[0]),
        pltpu.make_async_copy(keys_hbm, keys, load_sem.at[1]),
        pltpu.make_async_copy(win_hbm, win, load_sem.at[2]),
        pltpu.make_async_copy(wout_hbm, wout, load_sem.at[3]),
        pltpu.make_async_copy(proj_hbm, proj, load_sem.at[4]),
    ]
    loads[0].start()
    loads[1].start()

    barrier = pltpu.get_barrier_semaphore()
    for d in range(1, nt):
        pl.semaphore_signal(barrier, inc=1, device_id=at_tok(lax.rem(t + d, nt)), device_id_type=MESH)
    for d in range(1, nf):
        pl.semaphore_signal(barrier, inc=1, device_id=at_fc(lax.rem(f + d, nf)), device_id_type=MESH)

    def remote(src, dst, ss, rs, dev):
        return pltpu.make_async_remote_copy(
            src_ref=src, dst_ref=dst, send_sem=ss, recv_sem=rs, device_id=dev, device_id_type=MESH
        )

    loads[0].wait()
    pl.semaphore_wait(barrier, nt + nf - 2)

    def halo_low(p):
        return remote(
            cells.at[8 + p], cells.at[p], halo_ss.at[0, p], halo_rs.at[0, p], at_tok(t + 1)
        )

    def halo_high(p):
        return remote(
            cells.at[3 + p], cells.at[11 + p], halo_ss.at[1, p], halo_rs.at[1, p], at_tok(t - 1)
        )

    @pl.when(h == 0)
    def _():
        for p in range(3):
            halo_low(p).start()

    @pl.when(h == 1)
    def _():
        for p in range(3):
            halo_high(p).start()

    def start_cross(parts):
        @pl.when(jnp.logical_and(h == 1, t < nt - 1))
        def _():
            for p in parts:
                halo_low(p).start()

        @pl.when(jnp.logical_and(h == 0, t > 0))
        def _():
            for p in parts:
                halo_high(p).start()

    loads[1].wait()
    for c in loads[2:]:
        c.start()

    def logits_of(v):
        normed = rms_scale(v.astype(F32), ngain_ref[...]).astype(BF)
        return jnp.dot(normed, keys[...], preferred_element_type=F32)

    def softmax_of(l):
        e = jnp.exp(l - jnp.max(l, axis=-1, keepdims=True))
        return (e / jnp.sum(e, axis=-1, keepdims=True)).astype(BF)

    def first(r, peak):
        v = cells[pl.ds(3 + 2 * r, 2)].reshape(256, width)
        l = logits_of(v)
        logits[pl.ds(2 * r, 2)] = l.reshape(2, 128, width)
        return jnp.maximum(peak, jnp.max(l.reshape(32, 8, width), axis=0))

    def wait_low():
        @pl.when(t > 0)
        def _():
            for p in range(3):
                halo_low(p).wait_recv()

    def wait_high():
        @pl.when(t < nt - 1)
        def _():
            for p in range(3):
                halo_high(p).wait_recv()

    def halo_combine(cross):
        if cross:
            pl.when(h == 0)(wait_low)
            pl.when(h == 1)(wait_high)
            at = pl.ds(11 * h, 3)
        else:
            pl.when(h == 1)(wait_low)
            pl.when(h == 0)(wait_high)
            at = pl.ds(11 * (1 - h), 3)
        combine[at] = softmax_of(logits_of(cells[at].reshape(384, width))).reshape(3, 128, width)

    peak = lax.fori_loop(0, 4, first, jnp.full((8, width), -jnp.inf, F32))
    mine = jnp.max(peak, axis=0, keepdims=True)
    peaks[x] = mine
    peak_copies = []
    for d in range(1, 4):
        k = lax.rem(x + d, 4)
        c = remote(peaks.at[x], peaks.at[x], peak_ss.at[d - 1], peak_rs.at[d - 1], at_tok(k * 2 + h))
        c.start()
        peak_copies.append(c)

    @pl.when(t == 0)
    def _():
        cells[pl.ds(0, 3)] = jnp.zeros((3, 128, width), BF)

    @pl.when(t == nt - 1)
    def _():
        cells[pl.ds(11, 3)] = jnp.zeros((3, 128, width), BF)


    @pl.loop(0, 8)
    def _(r):
        shifted = jnp.exp(logits[r] - mine)
        disp[:, pl.ds(pl.multiple_of(r * 128, 128), 128)] = shifted.T.astype(BF)

    @pl.loop(0, 8)
    def _(r):
        combine[3 + r] = softmax_of(logits[r])

    for c in peak_copies:
        c.wait_recv()
    top = jnp.maximum(jnp.maximum(peaks[0], peaks[1]), jnp.maximum(peaks[2], peaks[3]))
    tops[h] = top
    top_copy = remote(tops.at[h], tops.at[h], top_ss, top_rs, to_pair)
    top_copy.start()

    def as_column(row):
        return jnp.broadcast_to(row, (128, width)).T

    shrink[...] = as_column(jnp.exp(mine - top)).reshape(nf, 4, 16, 128)

    w_copies, x_copies = [], []

    def pass_on(n):
        lane = pl.ds(n * cw, cw)
        for c in w_copies[n]:
            c.wait_recv()
        numer[0:8, right, :, lane] = (
            numer[0:8, right, :, lane].astype(F32) + passed[0, :, :, lane].astype(F32)
        ).astype(BF)
        numer[8:16, left, :, lane] = (
            numer[8:16, left, :, lane].astype(F32) + passed[1, :, :, lane].astype(F32)
        ).astype(BF)
        row = [
            remote(numer.at[:, right, :, lane], rx.at[0, :, :, lane], x_ss.at[n, 0], x_rs.at[n, 0], to_right),
            remote(numer.at[:, left, :, lane], rx.at[1, :, :, lane], x_ss.at[n, 1], x_rs.at[n, 1], to_left),
        ]
        for c in row:
            c.start()
        x_copies.append(row)

    for n in range(NCH):
        lane = pl.ds(n * cw, cw)
        own = cells[pl.ds(3, 8), :, lane].reshape(1024, cw)
        factor = shrink[...].reshape(1024, 128)
        numer[:, :, :, lane] = (
            jnp.dot(disp[...], own, preferred_element_type=F32) * jnp.concatenate([factor] * (cw // 128), axis=1)
        ).astype(BF).reshape(nf, 4, 16, cw)
        low = pl.ds(0, 8)
        high = pl.ds(8, 8)
        row = [
            remote(
                numer.at[low, across, :, lane], passed.at[0, :, :, lane], w_ss.at[n, 0], w_rs.at[n, 0], to_right
            ),
            remote(
                numer.at[high, across, :, lane], passed.at[1, :, :, lane], w_ss.at[n, 1], w_rs.at[n, 1], to_left
            ),
        ]
        for c in row:
            c.start()
        w_copies.append(row)
        if n > 0:
            pass_on(n - 1)
    pass_on(NCH - 1)

    y_copies = []
    for n in range(NCH):
        lane = pl.ds(n * cw, cw)
        for c in x_copies[n]:
            c.wait_recv()
        total = numer[:, x, :, lane].astype(F32)
        for d in range(2):
            total = total + rx[d, :, :, lane].astype(F32)
        low = total[:, 0:8].reshape(nf * 8, cw)
        high = total[:, 8:16].reshape(nf * 8, cw)
        ysend[:, lane] = jnp.where(h == 0, high, low).astype(BF)
        keep[:, lane] = jnp.where(h == 0, low, high)
        c = remote(ysend.at[:, lane], yrecv.at[:, lane], y_ss.at[n], y_rs.at[n], to_pair)
        c.start()
        y_copies.append(c)

    top_copy.wait_recv()
    whole = jnp.maximum(tops[0], tops[1])

    def my_slots(row):
        shrink[...] = as_column(row).reshape(nf, 4, 16, 128)
        both = shrink[:, x]
        picked = jnp.where(h == 0, both[:, 0:8], both[:, 8:16]).reshape(nf * 8, 128)
        return jnp.concatenate([picked] * (width // 128), axis=1)

    keep[...] = keep[...] * my_slots(jnp.exp(tops[h] - whole))
    other = my_slots(jnp.exp(tops[1 - h] - whole))
    for c in y_copies:
        c.wait_recv()
    local_in = rms_scale(keep[...] + yrecv[...].astype(F32) * other, sgain_ref[...])
    asend[...] = fold_halves(local_in.reshape(nf, 8, width)).astype(BF)
    arecv[f] = asend[f]
    a_copies = []
    for d in range(1, nf):
        k = lax.rem(f + d, nf)
        c = remote(asend.at[k], arecv.at[f], a_ss.at[d - 1], a_rs.at[d - 1], at_fc(k))
        c.start()
        a_copies.append(c)
    start_cross(AT_SEND)
    halo_combine(False)
    loads[2].wait()
    loads[3].wait()
    for c in a_copies:
        c.wait_recv()

    lhs = unfold_halves(arecv[...].astype(F32)).reshape(nf * 8, width).astype(BF)
    which = lax.rem(lax.broadcasted_iota(jnp.int32, (nf * 8, 1), 0), 8) < 4
    hid = jnp.where(
        which,
        jnp.dot(lhs, win[0], preferred_element_type=F32),
        jnp.dot(lhs, win[1], preferred_element_type=F32),
    )
    hid = jax.nn.gelu(hid).astype(BF)
    out = jnp.where(
        which,
        jnp.dot(hid, wout[0], preferred_element_type=F32),
        jnp.dot(hid, wout[1], preferred_element_type=F32),
    )
    bsend[...] = out.reshape(nf, 8, width).astype(BF)
    every[t, f] = bsend[f]
    b_copies = []
    for d in range(1, nf):
        k = lax.rem(f + d, nf)
        c = remote(bsend.at[k], every.at[t, f], b_ss.at[d - 1], b_rs.at[d - 1], at_fc(k))
        c.start()
        b_copies.append(c)
    start_cross(AT_RETURN)
    for c in b_copies:
        c.wait_recv()

    sides = ((h, t), (1 - h, x * 2 + 1 - h))
    pair_copies = []
    for n in range(NCH):
        ref = every.at[t, :, :, pl.ds(n * cw, cw)]
        c = remote(ref, ref, p_ss.at[n], p_rs.at[n], to_pair)
        c.start()
        pair_copies.append(c)
    g_copies, o_copies = {}, {}

    def send_out(b, n):
        if b == 1:
            pair_copies[n].wait_recv()
        ref = every.at[sides[b][1], :, :, pl.ds(n * cw, cw)]
        g_copies[b, n] = [
            remote(ref, ref, g_ss.at[b, n, 0], g_rs.at[b, n, 0], to_right),
            remote(ref, ref, g_ss.at[b, n, 1], g_rs.at[b, n, 1], to_left),
        ]
        for c in g_copies[b, n]:
            c.start()

    def forward(b, n):
        lane = pl.ds(n * cw, cw)
        g_copies[b, n][0].wait_recv()
        ref = every.at[left * 2 + sides[b][0], pl.ds(0, 8), :, lane]
        go = remote(ref, ref, o_ss.at[b, n, 0], o_rs.at[b, n, 0], to_right)
        go.start()
        g_copies[b, n][1].wait_recv()
        ref = every.at[right * 2 + sides[b][0], pl.ds(8, 8), :, lane]
        back = remote(ref, ref, o_ss.at[b, n, 1], o_rs.at[b, n, 1], to_left)
        back.start()
        o_copies[b, n] = [go, back]

    rows = 7 * 128

    def mix(n):
        lane = pl.ds(n * cw, cw)
        for b in range(2):
            for c in o_copies[b, n]:
                c.wait_recv()
        joined[...] = jnp.concatenate(
            [every[tt, ff, :, lane].astype(F32) for ff in range(nf) for tt in range(nt)], axis=0
        ).astype(BF)

        @pl.loop(0, 2)
        def _(b):
            mixed = jnp.dot(
                combine[pl.ds(b * 7, 7)].reshape(rows, width), joined[...], preferred_element_type=F32
            )
            v = cells[pl.ds(b * 7, 7), :, lane].reshape(rows, cw).astype(F32) + mixed
            at = lax.broadcasted_iota(jnp.int32, (rows, 1), 0) + (b * rows + (8 * t - 3) * 128)
            inside = jnp.logical_and(at >= 0, at < 64 * 128)
            v = jnp.where(inside, v, 0.0)
            state[pl.ds(b * 7, 7), :, lane] = v.astype(BF).reshape(7, 128, cw)

    def convolve(k):
        lane = pl.ds(k * 128, 128)
        for tap in range(49):
            row = cw_ref[tap // 7, pl.ds(tap % 7, 1), lane]
            taps[tap] = jnp.broadcast_to(row, (16, 128)).astype(BF)

        @pl.loop(0, 14)
        def _(r):
            v = state[r, :, lane].astype(F32)
            wide[r, pl.ds(8, 128), :] = v
            wide[r, pl.ds(0, 8), :] = v[120:128]
            wide[r, pl.ds(136, 8), :] = v[0:8]

        @pl.loop(0, 8)
        def _(i):
            acc = [[None] * 4, [None] * 4]
            for b in range(7):
                wv = [taps[a * 7 + b] for a in range(7)]
                for blk in range(2):
                    start = i * 16 + (8 * blk + 5 + b)
                    v = [wide[r, pl.ds(start, 8), :] for r in range(14)]
                    pk = [jnp.concatenate([v[q], v[q + 4]], axis=0).astype(BF) for q in range(10)]
                    for p in range(4):
                        term = tree_sum(pk[p + a] * wv[a] for a in range(7))
                        acc[blk][p] = term if acc[blk][p] is None else acc[blk][p] + term
            for blk in range(2):
                for p in range(4):
                    val = acc[blk][p].astype(F32)
                    at = pl.multiple_of(i * 16 + 8 * blk, 8)
                    conv[p, pl.ds(at, 8), lane] = val[0:8]
                    conv[p + 4, pl.ds(at, 8), lane] = val[8:16]

    send_out(0, 0)
    send_out(0, 1)
    start_cross(LATE)
    send_out(1, 0)
    forward(0, 0)
    send_out(0, 2)
    send_out(1, 1)
    forward(1, 0)
    forward(0, 1)
    halo_combine(True)
    mix(0)
    send_out(0, 3)
    send_out(1, 2)
    forward(1, 1)
    forward(0, 2)
    convolve(0)
    send_out(1, 3)
    forward(1, 2)
    forward(0, 3)
    convolve(1)
    mix(1)
    forward(1, 3)
    convolve(2)
    convolve(3)
    mix(2)
    convolve(4)
    convolve(5)
    mix(3)
    convolve(6)
    convolve(7)
    loads[4].wait()

    def norm_row(r, into):
        c = conv[r]
        center = c - jnp.mean(c, axis=-1, keepdims=True)
        spread = jnp.mean(center * center, axis=-1, keepdims=True)
        into[...] = (center * lax.rsqrt(spread + 1e-06) * lgain_ref[...]).astype(BF)

    def finish_row(r, source):
        branch = jnp.dot(source[...], proj[...], preferred_element_type=F32)
        res = state[r + 3].astype(F32) + scale_ref[...] * jax.nn.gelu(branch)
        outs[r] = res.astype(BF)
        pltpu.make_async_copy(outs.at[r], out_hbm.at[r], out_sem.at[r]).start()

    norm_row(0, even)

    @pl.loop(0, 4)
    def _(i):
        norm_row(2 * i + 1, odd)
        finish_row(2 * i, even)
        norm_row(jnp.minimum(2 * i + 2, 7), even)
        finish_row(2 * i + 1, odd)

    sent = peak_copies + y_copies + a_copies + b_copies + pair_copies + [top_copy]
    for group in (w_copies, x_copies, g_copies.values(), o_copies.values()):
        sent += [c for row in group for c in row]
    for c in sent:
        c.wait_send()

    @pl.when(t < nt - 1)
    def _():
        for p in range(3):
            halo_low(p).wait_send()

    @pl.when(t > 0)
    def _():
        for p in range(3):
            halo_high(p).wait_send()

    for r in range(8):
        pltpu.make_async_copy(outs.at[r], out_hbm.at[r], out_sem.at[r]).wait()


def fused(
    tokens, slot_keys, norm_gain, slot_gain, w_in, w_out, conv_weight, ln_gain, proj, layer_scale
):
    width = tokens.shape[2]
    vm = pl.BlockSpec(memory_space=pltpu.VMEM)
    anyspec = pl.BlockSpec(memory_space=pl.ANY)
    dma = pltpu.SemaphoreType.DMA
    nf = MEMBERS_AX
    return pl.pallas_call(
        mix_kernel,
        out_shape=jax.ShapeDtypeStruct((8, 128, width), BF),
        in_specs=[anyspec, anyspec, vm, vm, anyspec, anyspec, vm, vm, vm, anyspec],
        out_specs=anyspec,
        scratch_shapes=[
            pltpu.VMEM((14, 128, width), BF),
            pltpu.VMEM((width, width), BF),
            pltpu.VMEM(w_in.shape, BF),
            pltpu.VMEM(w_out.shape, BF),
            pltpu.VMEM((8, 128, width), F32),
            pltpu.VMEM((14, 128, width), BF),
            pltpu.VMEM((width, 1024), BF),
            pltpu.VMEM((nf, 4, 16, width), BF),
            pltpu.VMEM((2, 8, 16, width), BF),
            pltpu.VMEM((2, nf, 16, width), BF),
            pltpu.VMEM((nf * 8, width), BF),
            pltpu.VMEM((nf * 8, width), BF),
            pltpu.VMEM((nf * 8, width), F32),
            pltpu.VMEM((nf, 16, width // 2), BF),
            pltpu.VMEM((nf, 16, width // 2), BF),
            pltpu.VMEM((nf, 8, width), BF),
            pltpu.VMEM((8, nf, 8, width), BF),
            pltpu.VMEM((1024, width // NCH), BF),
            pltpu.VMEM((14, 128, width), BF),
            pltpu.VMEM((14, 144, 128), F32),
            pltpu.VMEM((49, 16, 128), BF),
            pltpu.VMEM((8, 128, width), F32),
            pltpu.VMEM((128, width), BF),
            pltpu.VMEM((128, width), BF),
            pltpu.VMEM((8, 128, width), BF),
            pltpu.VMEM((width, width), BF),
            pltpu.VMEM((4, 1, width), F32),
            pltpu.VMEM((2, 1, width), F32),
            pltpu.VMEM((nf, 4, 16, 128), F32),
            dma((5,)),
            dma((3,)), dma((3,)),
            dma, dma,
            dma((2, 3)), dma((2, 3)),
            dma((NCH, 2)), dma((NCH, 2)),
            dma((NCH, 2)), dma((NCH, 2)),
            dma((NCH,)), dma((NCH,)),
            dma((15,)), dma((15,)),
            dma((15,)), dma((15,)),
            dma((NCH,)), dma((NCH,)),
            dma((2, NCH, 2)), dma((2, NCH, 2)),
            dma((2, NCH, 2)), dma((2, NCH, 2)),
            dma((8,)),
        ],
        compiler_params=pltpu.CompilerParams(
            collective_id=0, has_side_effects=True, vmem_limit_bytes=62 * 1024 * 1024
        ),
        name="fused",
    )(
        tokens, slot_keys, norm_gain.reshape(1, width), slot_gain.reshape(1, width), w_in, w_out,
        conv_weight, ln_gain.reshape(1, width), layer_scale.reshape(1, width), proj,
    )


def tree_sum(terms):
    terms = list(terms)
    while len(terms) > 1:
        nxt = [terms[i] + terms[i + 1] for i in range(0, len(terms) - 1, 2)]
        if len(terms) % 2:
            nxt.append(terms[-1])
        terms = nxt
    return terms[0]


def local(
    tokens, slot_keys, norm_gain, slot_gain, w_in, w_out, conv_weight, ln_gain, proj, layer_scale
):
    return fused(
        tokens[0], slot_keys, norm_gain, slot_gain, w_in, w_out, conv_weight, ln_gain, proj, layer_scale
    )[None]


def solution(mesh):
    in_specs = (
        P("fc", "tok", None, None),
        P(),
        P(),
        P(),
        P(("fc", "tok"), None, None),
        P(("fc", "tok"), None, None),
        P(),
        P(),
        P(),
        P(),
    )
    out_specs = P("fc", "tok", None, None)
    return jax.shard_map(local, mesh=mesh, in_specs=in_specs, out_specs=out_specs, check_vma=False)
```

time: 127 us -> 119 us (0.937)
  Pallas kernels: 125 us -> 115 us
  local copies, waits for them, and re-layouts: 1.66 us -> 3.08 us
    pallas_call x2 -> x1, Pallas kernels: 125 us -> 115 us  [fused(): pl.pallas_call(mix_kernel, out_shape=jax.ShapeDtypeStruct((8, 128, width)...]
    unnamed x0 -> x1, local copies, waits for them, and re-layouts: none -> 3.08 us
    reshape x1 -> x0, local copies, waits for them, and re-layouts: 1.66 us -> none  [block(): conv_weight.reshape(49, width)]
where the time goes in v3:
time: 119 us; the launch traced here: 118 us
  Pallas kernels  115 us (97%)
  local copies, waits for them, and re-layouts  3.08 us (3%)
    pallas_call x1, Pallas kernels, fused(): pl.pallas_call(mix_kernel, out_shape=jax.ShapeDtypeStruct((8, 128, width)...  115 us
    unnamed x1, local copies, waits for them, and re-layouts  3.08 us

profile of v3, /device:TPU:0, one launch (start us, length us, event | category | flops | bytes accessed | tf_op | source)
XLA Modules:
  0.0 118.2 jit_solution(17230398961650104611)
XLA Ops:
  0.0 115.1 %fused.1 = bf16[8,128,1024]{2,1,0:T(8,128)(2,1)} custom-call(bf16[8,128,1024]{2,1,0:T(8,128)(2,1)} %bitcast.7, bf16[1024,1024]{1,0:T(8,128)(2,1)} %keys_hbm.1, f32[1,1024]{1,0:T(1,128)} %bitcast.8, f32[1,1024]{1,0:T(1,128)} %bitcast.9, bf16[2,1024,512]{2,1,0:T(8,128)(2,1)} %win_hbm.1, bf16[2,512,1024]{2,1,0:T(8,128)(2,1)} %wout_hbm.1, f32[7,7,1024]{2,1,0:T(8,128)} %cw_ref.1, ...), custom_call_target="tpu_custom_call" | custom-call | tf_op jit(solution)/shard_map/fused/pallas_call | solution.py:472
  115.1 3.1 %copy.12 = bf16[1,8,128,1024]{3,2,1,0:T(8,128)(2,1)} copy(bf16[1,8,128,1024]{3,2,1,0:T(8,128)(2,1)} %bitcast.6) | data formatting | bytes 4194304

commit v4 on v3

--- a/solution.py
+++ b/solution.py
@@ -10,7 +10,7 @@
 MESH = pl.DeviceIdType.MESH
 MEMBERS_AX = 16
 NCH = 4
-AT_SEND, AT_RETURN, LATE = (0,), (1,), (2,)
+FIRST, EARLY, AT_EXPERT, LATE = (0,), (1,), (), (2,)
 
 
 def rms_scale(value, gain):
@@ -33,7 +33,7 @@
     cells, keys, win, wout, logits, combine, disp, numer, passed, rx, ysend, yrecv, keep,
     asend, arecv, bsend, every, joined, state, wide, taps, conv, even, odd, outs, proj, peaks, tops, shrink, load_sem,
     peak_ss, peak_rs, top_ss, top_rs, halo_ss, halo_rs, w_ss, w_rs, x_ss, x_rs, y_ss, y_rs, a_ss, a_rs, b_ss, b_rs,
-    p_ss, p_rs, g_ss, g_rs, o_ss, o_rs, out_sem,
+    p_ss, p_rs, g_ss, g_rs, out_sem,
 ):
     nf, nt = MEMBERS_AX, 8
     width = cells.shape[2]
@@ -74,7 +74,6 @@
         )
 
     loads[0].wait()
-    pl.semaphore_wait(barrier, nt + nf - 2)
 
     def halo_low(p):
         return remote(
@@ -85,16 +84,6 @@
         return remote(
             cells.at[3 + p], cells.at[11 + p], halo_ss.at[1, p], halo_rs.at[1, p], at_tok(t - 1)
         )
-
-    @pl.when(h == 0)
-    def _():
-        for p in range(3):
-            halo_low(p).start()
-
-    @pl.when(h == 1)
-    def _():
-        for p in range(3):
-            halo_high(p).start()
 
     def start_cross(parts):
         @pl.when(jnp.logical_and(h == 1, t < nt - 1))
@@ -125,30 +114,30 @@
         logits[pl.ds(2 * r, 2)] = l.reshape(2, 128, width)
         return jnp.maximum(peak, jnp.max(l.reshape(32, 8, width), axis=0))
 
-    def wait_low():
-        @pl.when(t > 0)
-        def _():
-            for p in range(3):
-                halo_low(p).wait_recv()
-
-    def wait_high():
-        @pl.when(t < nt - 1)
-        def _():
-            for p in range(3):
-                halo_high(p).wait_recv()
-
-    def halo_combine(cross):
-        if cross:
-            pl.when(h == 0)(wait_low)
-            pl.when(h == 1)(wait_high)
-            at = pl.ds(11 * h, 3)
-        else:
-            pl.when(h == 1)(wait_low)
-            pl.when(h == 0)(wait_high)
-            at = pl.ds(11 * (1 - h), 3)
-        combine[at] = softmax_of(logits_of(cells[at].reshape(384, width))).reshape(3, 128, width)
-
-    peak = lax.fori_loop(0, 4, first, jnp.full((8, width), -jnp.inf, F32))
+    def halo_combine(cross, start, count):
+        def wait_low():
+            @pl.when(t > 0)
+            def _():
+                for p in range(start, start + count):
+                    halo_low(p).wait_recv()
+
+        def wait_high():
+            @pl.when(t < nt - 1)
+            def _():
+                for p in range(start, start + count):
+                    halo_high(p).wait_recv()
+
+        pl.when(h == (0 if cross else 1))(wait_low)
+        pl.when(h == (1 if cross else 0))(wait_high)
+        at = pl.ds(11 * (h if cross else 1 - h) + start, count)
+        rows_in = cells[at].reshape(count * 128, width)
+        combine[at] = softmax_of(logits_of(rows_in)).reshape(count, 128, width)
+
+    peak = lax.fori_loop(0, 2, first, jnp.full((8, width), -jnp.inf, F32))
+    pl.semaphore_wait(barrier, nt + nf - 2)
+
+    start_cross(FIRST)
+    peak = lax.fori_loop(2, 4, first, peak)
     mine = jnp.max(peak, axis=0, keepdims=True)
     peaks[x] = mine
     peak_copies = []
@@ -158,6 +147,16 @@
         c.start()
         peak_copies.append(c)
 
+    @pl.when(h == 0)
+    def _():
+        for p in range(3):
+            halo_low(p).start()
+
+    @pl.when(h == 1)
+    def _():
+        for p in range(3):
+            halo_high(p).start()
+
     @pl.when(t == 0)
     def _():
         cells[pl.ds(0, 3)] = jnp.zeros((3, 128, width), BF)
@@ -178,6 +177,7 @@
 
     for c in peak_copies:
         c.wait_recv()
+    start_cross(EARLY)
     top = jnp.maximum(jnp.maximum(peaks[0], peaks[1]), jnp.maximum(peaks[2], peaks[3]))
     tops[h] = top
     top_copy = remote(tops.at[h], tops.at[h], top_ss, top_rs, to_pair)
@@ -270,13 +270,13 @@
         c = remote(asend.at[k], arecv.at[f], a_ss.at[d - 1], a_rs.at[d - 1], at_fc(k))
         c.start()
         a_copies.append(c)
-    start_cross(AT_SEND)
-    halo_combine(False)
+    halo_combine(False, 0, 3)
     loads[2].wait()
     loads[3].wait()
     for c in a_copies:
         c.wait_recv()
 
+    start_cross(AT_EXPERT)
     lhs = unfold_halves(arecv[...].astype(F32)).reshape(nf * 8, width).astype(BF)
     which = lax.rem(lax.broadcasted_iota(jnp.int32, (nf * 8, 1), 0), 8) < 4
     hid = jnp.where(
@@ -298,7 +298,7 @@
         c = remote(bsend.at[k], every.at[t, f], b_ss.at[d - 1], b_rs.at[d - 1], at_fc(k))
         c.start()
         b_copies.append(c)
-    start_cross(AT_RETURN)
+    halo_combine(True, 0, 2)
     for c in b_copies:
         c.wait_recv()
 
@@ -309,38 +309,28 @@
         c = remote(ref, ref, p_ss.at[n], p_rs.at[n], to_pair)
         c.start()
         pair_copies.append(c)
-    g_copies, o_copies = {}, {}
+        if n == 1:
+            start_cross(LATE)
+    g_copies = {}
 
     def send_out(b, n):
         if b == 1:
             pair_copies[n].wait_recv()
         ref = every.at[sides[b][1], :, :, pl.ds(n * cw, cw)]
-        g_copies[b, n] = [
-            remote(ref, ref, g_ss.at[b, n, 0], g_rs.at[b, n, 0], to_right),
-            remote(ref, ref, g_ss.at[b, n, 1], g_rs.at[b, n, 1], to_left),
-        ]
-        for c in g_copies[b, n]:
+        g_copies[b, n] = []
+        for d in (1, 3, 2):
+            c = remote(
+                ref, ref, g_ss.at[b, n, d - 1], g_rs.at[b, n, d - 1], at_tok(lax.rem(x + d, 4) * 2 + h)
+            )
             c.start()
-
-    def forward(b, n):
-        lane = pl.ds(n * cw, cw)
-        g_copies[b, n][0].wait_recv()
-        ref = every.at[left * 2 + sides[b][0], pl.ds(0, 8), :, lane]
-        go = remote(ref, ref, o_ss.at[b, n, 0], o_rs.at[b, n, 0], to_right)
-        go.start()
-        g_copies[b, n][1].wait_recv()
-        ref = every.at[right * 2 + sides[b][0], pl.ds(8, 8), :, lane]
-        back = remote(ref, ref, o_ss.at[b, n, 1], o_rs.at[b, n, 1], to_left)
-        back.start()
-        o_copies[b, n] = [go, back]
+            g_copies[b, n].append(c)
 
     rows = 7 * 128
 
     def mix(n):
         lane = pl.ds(n * cw, cw)
-        for b in range(2):
-            for c in o_copies[b, n]:
-                c.wait_recv()
+        for c in g_copies[0, n] + g_copies[1, n]:
+            c.wait_recv()
         joined[...] = jnp.concatenate(
             [every[tt, ff, :, lane].astype(F32) for ff in range(nf) for tt in range(nt)], axis=0
         ).astype(BF)
@@ -390,26 +380,17 @@
 
     send_out(0, 0)
     send_out(0, 1)
-    start_cross(LATE)
     send_out(1, 0)
-    forward(0, 0)
+    send_out(1, 1)
     send_out(0, 2)
-    send_out(1, 1)
-    forward(1, 0)
-    forward(0, 1)
-    halo_combine(True)
+    halo_combine(True, 2, 1)
+    send_out(1, 2)
+    send_out(0, 3)
+    send_out(1, 3)
     mix(0)
-    send_out(0, 3)
-    send_out(1, 2)
-    forward(1, 1)
-    forward(0, 2)
     convolve(0)
-    send_out(1, 3)
-    forward(1, 2)
-    forward(0, 3)
     convolve(1)
     mix(1)
-    forward(1, 3)
     convolve(2)
     convolve(3)
     mix(2)
@@ -442,7 +423,7 @@
         finish_row(2 * i + 1, odd)
 
     sent = peak_copies + y_copies + a_copies + b_copies + pair_copies + [top_copy]
-    for group in (w_copies, x_copies, g_copies.values(), o_copies.values()):
+    for group in (w_copies, x_copies, g_copies.values()):
         sent += [c for row in group for c in row]
     for c in sent:
         c.wait_send()
@@ -514,8 +495,7 @@
             dma((15,)), dma((15,)),
             dma((15,)), dma((15,)),
             dma((NCH,)), dma((NCH,)),
-            dma((2, NCH, 2)), dma((2, NCH, 2)),
-            dma((2, NCH, 2)), dma((2, NCH, 2)),
+            dma((2, NCH, 3)), dma((2, NCH, 3)),
             dma((8,)),
         ],
         compiler_params=pltpu.CompilerParams(

time: 119 us -> 103 us (0.87)
  Pallas kernels: 115 us -> 98.9 us
    pallas_call x1, Pallas kernels: 115 us -> 98.9 us  [fused(): pl.pallas_call(mix_kernel, out_shape=jax.ShapeDtypeStruct((8, 128, width)...]
where the time goes in v4:
time: 103 us; the launch traced here: 102 us
  Pallas kernels  98.9 us (96%)
  local copies, waits for them, and re-layouts  3.08 us (3%)
    pallas_call x1, Pallas kernels, fused(): pl.pallas_call(mix_kernel, out_shape=jax.ShapeDtypeStruct((8, 128, width)...  98.9 us
    unnamed x1, local copies, waits for them, and re-layouts  3.08 us

profile of v4, /device:TPU:0, one launch (start us, length us, event | category | flops | bytes accessed | tf_op | source)
XLA Modules:
  0.0 102.0 jit_solution(3004805865990165242)
XLA Ops:
  0.0 98.9 %fused.1 = bf16[8,128,1024]{2,1,0:T(8,128)(2,1)} custom-call(bf16[8,128,1024]{2,1,0:T(8,128)(2,1)} %bitcast.7, bf16[1024,1024]{1,0:T(8,128)(2,1)} %keys_hbm.1, f32[1,1024]{1,0:T(1,128)} %bitcast.8, f32[1,1024]{1,0:T(1,128)} %bitcast.9, bf16[2,1024,512]{2,1,0:T(8,128)(2,1)} %win_hbm.1, bf16[2,512,1024]{2,1,0:T(8,128)(2,1)} %wout_hbm.1, f32[7,7,1024]{2,1,0:T(8,128)} %cw_ref.1, ...), custom_call_target="tpu_custom_call" | custom-call | tf_op jit(solution)/shard_map/fused/pallas_call | solution.py:453
  98.9 3.1 %copy.12 = bf16[1,8,128,1024]{3,2,1,0:T(8,128)(2,1)} copy(bf16[1,8,128,1024]{3,2,1,0:T(8,128)(2,1)} %bitcast.6) | data formatting | bytes 4194304

commit v5 on v4

--- a/solution.py
+++ b/solution.py
@@ -10,7 +10,7 @@
 MESH = pl.DeviceIdType.MESH
 MEMBERS_AX = 16
 NCH = 4
-FIRST, EARLY, AT_EXPERT, LATE = (0,), (1,), (), (2,)
+FIRST, EARLY, LAST = (2,), (1,), (0,)
 
 
 def rms_scale(value, gain):
@@ -94,7 +94,7 @@
         @pl.when(jnp.logical_and(h == 0, t > 0))
         def _():
             for p in parts:
-                halo_high(p).start()
+                halo_high(2 - p).start()
 
     loads[1].wait()
     for c in loads[2:]:
@@ -114,24 +114,34 @@
         logits[pl.ds(2 * r, 2)] = l.reshape(2, 128, width)
         return jnp.maximum(peak, jnp.max(l.reshape(32, 8, width), axis=0))
 
-    def halo_combine(cross, start, count):
-        def wait_low():
-            @pl.when(t > 0)
-            def _():
-                for p in range(start, start + count):
-                    halo_low(p).wait_recv()
-
-        def wait_high():
-            @pl.when(t < nt - 1)
-            def _():
-                for p in range(start, start + count):
-                    halo_high(p).wait_recv()
-
-        pl.when(h == (0 if cross else 1))(wait_low)
-        pl.when(h == (1 if cross else 0))(wait_high)
-        at = pl.ds(11 * (h if cross else 1 - h) + start, count)
-        rows_in = cells[at].reshape(count * 128, width)
-        combine[at] = softmax_of(logits_of(rows_in)).reshape(count, 128, width)
+    def pure_combine():
+        @pl.when(h == 1)
+        def _():
+            for p in range(3):
+                halo_low(p).wait_recv()
+
+        @pl.when(h == 0)
+        def _():
+            for p in range(3):
+                halo_high(p).wait_recv()
+
+        at = pl.ds(11 * (1 - h), 3)
+        rows_in = cells[at].reshape(384, width)
+        combine[at] = softmax_of(logits_of(rows_in)).reshape(3, 128, width)
+
+    def cross_at(p):
+        return p + h * (13 - 2 * p)
+
+    def cross_combine(p):
+        @pl.when(jnp.logical_and(h == 0, t > 0))
+        def _():
+            halo_low(p).wait_recv()
+
+        @pl.when(jnp.logical_and(h == 1, t < nt - 1))
+        def _():
+            halo_high(2 - p).wait_recv()
+
+        combine[cross_at(p)] = softmax_of(logits_of(cells[cross_at(p)]))
 
     peak = lax.fori_loop(0, 2, first, jnp.full((8, width), -jnp.inf, F32))
     pl.semaphore_wait(barrier, nt + nf - 2)
@@ -270,13 +280,12 @@
         c = remote(asend.at[k], arecv.at[f], a_ss.at[d - 1], a_rs.at[d - 1], at_fc(k))
         c.start()
         a_copies.append(c)
-    halo_combine(False, 0, 3)
+    pure_combine()
     loads[2].wait()
     loads[3].wait()
     for c in a_copies:
         c.wait_recv()
 
-    start_cross(AT_EXPERT)
     lhs = unfold_halves(arecv[...].astype(F32)).reshape(nf * 8, width).astype(BF)
     which = lax.rem(lax.broadcasted_iota(jnp.int32, (nf * 8, 1), 0), 8) < 4
     hid = jnp.where(
@@ -298,7 +307,8 @@
         c = remote(bsend.at[k], every.at[t, f], b_ss.at[d - 1], b_rs.at[d - 1], at_fc(k))
         c.start()
         b_copies.append(c)
-    halo_combine(True, 0, 2)
+    cross_combine(2)
+    cross_combine(1)
     for c in b_copies:
         c.wait_recv()
 
@@ -309,8 +319,6 @@
         c = remote(ref, ref, p_ss.at[n], p_rs.at[n], to_pair)
         c.start()
         pair_copies.append(c)
-        if n == 1:
-            start_cross(LATE)
     g_copies = {}
 
     def send_out(b, n):
@@ -325,26 +333,40 @@
             c.start()
             g_copies[b, n].append(c)
 
-    rows = 7 * 128
+    state[13 * h] = jnp.zeros((128, width), BF)
 
     def mix(n):
         lane = pl.ds(n * cw, cw)
         for c in g_copies[0, n] + g_copies[1, n]:
             c.wait_recv()
-        joined[...] = jnp.concatenate(
+        joined[n] = jnp.concatenate(
             [every[tt, ff, :, lane].astype(F32) for ff in range(nf) for tt in range(nt)], axis=0
         ).astype(BF)
-
-        @pl.loop(0, 2)
-        def _(b):
-            mixed = jnp.dot(
-                combine[pl.ds(b * 7, 7)].reshape(rows, width), joined[...], preferred_element_type=F32
-            )
-            v = cells[pl.ds(b * 7, 7), :, lane].reshape(rows, cw).astype(F32) + mixed
-            at = lax.broadcasted_iota(jnp.int32, (rows, 1), 0) + (b * rows + (8 * t - 3) * 128)
+        for base, count in ((0, 6), (6, 7)):
+            rows = count * 128
+            span = pl.ds(1 - h + base, count)
+            mixed = jnp.dot(combine[span].reshape(rows, width), joined[n], preferred_element_type=F32)
+            v = cells[span, :, lane].reshape(rows, cw).astype(F32) + mixed
+            at = lax.broadcasted_iota(jnp.int32, (rows, 1), 0) + (8 * t - 2 - h + base) * 128
             inside = jnp.logical_and(at >= 0, at < 64 * 128)
             v = jnp.where(inside, v, 0.0)
-            state[pl.ds(b * 7, 7), :, lane] = v.astype(BF).reshape(7, 128, cw)
+            state[span, :, lane] = v.astype(BF).reshape(count, 128, cw)
+
+    inner = jnp.where(h == 0, t > 0, t < nt - 1)
+
+    def add_far_row(n):
+        lane = pl.ds(n * cw, cw)
+        mixed = jnp.dot(combine[13 * h], joined[n], preferred_element_type=F32)
+        v = (cells[13 * h, :, lane].astype(F32) + mixed).astype(BF).astype(F32)
+        v = jnp.where(inner, v, 0.0)
+        for part in range(cw // 128):
+            u = v[:, part * 128 : (part + 1) * 128]
+            wide[part, pl.ds(8, 128), :] = u
+            wide[part, pl.ds(0, 8), :] = u[120:128]
+            wide[part, pl.ds(136, 8), :] = u[0:8]
+            here = pl.ds(n * cw + part * 128, 128)
+            terms = [wide[part, pl.ds(5 + b, 128), :] * cw_ref[6 * h, pl.ds(b, 1), here] for b in range(7)]
+            conv[7 * h, :, here] = conv[7 * h, :, here] + tree_sum(terms)
 
     def convolve(k):
         lane = pl.ds(k * 128, 128)
@@ -383,10 +405,10 @@
     send_out(1, 0)
     send_out(1, 1)
     send_out(0, 2)
-    halo_combine(True, 2, 1)
     send_out(1, 2)
     send_out(0, 3)
     send_out(1, 3)
+    start_cross(LAST)
     mix(0)
     convolve(0)
     convolve(1)
@@ -399,6 +421,9 @@
     mix(3)
     convolve(6)
     convolve(7)
+    cross_combine(0)
+    for n in range(NCH):
+        add_far_row(n)
     loads[4].wait()
 
     def norm_row(r, into):
@@ -473,7 +498,7 @@
             pltpu.VMEM((nf, 16, width // 2), BF),
             pltpu.VMEM((nf, 8, width), BF),
             pltpu.VMEM((8, nf, 8, width), BF),
-            pltpu.VMEM((1024, width // NCH), BF),
+            pltpu.VMEM((NCH, 1024, width // NCH), BF),
             pltpu.VMEM((14, 128, width), BF),
             pltpu.VMEM((14, 144, 128), F32),
             pltpu.VMEM((49, 16, 128), BF),

time: 103 us -> 100 us (0.971)
  Pallas kernels: 98.9 us -> 96 us
    pallas_call x1, Pallas kernels: 98.9 us -> 96 us  [fused(): pl.pallas_call(mix_kernel, out_shape=jax.ShapeDtypeStruct((8, 128, width)...]
where the time goes in v5:
time: 100 us; the launch traced here: 99.1 us
  Pallas kernels  96 us (96%)
  local copies, waits for them, and re-layouts  3.08 us (3%)
    pallas_call x1, Pallas kernels, fused(): pl.pallas_call(mix_kernel, out_shape=jax.ShapeDtypeStruct((8, 128, width)...  96 us
    unnamed x1, local copies, waits for them, and re-layouts  3.08 us

profile of v5, /device:TPU:0, one launch (start us, length us, event | category | flops | bytes accessed | tf_op | source)
XLA Modules:
  0.0 99.1 jit_solution(9830347143217328941)
XLA Ops:
  0.0 96.0 %fused.1 = bf16[8,128,1024]{2,1,0:T(8,128)(2,1)} custom-call(bf16[8,128,1024]{2,1,0:T(8,128)(2,1)} %bitcast.7, bf16[1024,1024]{1,0:T(8,128)(2,1)} %keys_hbm.1, f32[1,1024]{1,0:T(1,128)} %bitcast.8, f32[1,1024]{1,0:T(1,128)} %bitcast.9, bf16[2,1024,512]{2,1,0:T(8,128)(2,1)} %win_hbm.1, bf16[2,512,1024]{2,1,0:T(8,128)(2,1)} %wout_hbm.1, f32[7,7,1024]{2,1,0:T(8,128)} %cw_ref.1, ...), custom_call_target="tpu_custom_call" | custom-call | tf_op jit(solution)/shard_map/fused/pallas_call | solution.py:478
  96.0 3.1 %copy.12 = bf16[1,8,128,1024]{3,2,1,0:T(8,128)(2,1)} copy(bf16[1,8,128,1024]{3,2,1,0:T(8,128)(2,1)} %bitcast.6) | data formatting | bytes 4194304

commit v6 on v5

--- a/solution.py
+++ b/solution.py
@@ -187,7 +187,6 @@
 
     for c in peak_copies:
         c.wait_recv()
-    start_cross(EARLY)
     top = jnp.maximum(jnp.maximum(peaks[0], peaks[1]), jnp.maximum(peaks[2], peaks[3]))
     tops[h] = top
     top_copy = remote(tops.at[h], tops.at[h], top_ss, top_rs, to_pair)
@@ -241,6 +240,7 @@
         if n > 0:
             pass_on(n - 1)
     pass_on(NCH - 1)
+    start_cross(EARLY)
 
     y_copies = []
     for n in range(NCH):

time: 100 us -> 101 us (1.010)
  no operation moved by 1% of the time
where the time goes in v6:
time: 101 us; the launch traced here: 99.5 us
  Pallas kernels  96.5 us (96%)
  local copies, waits for them, and re-layouts  3.08 us (3%)
    pallas_call x1, Pallas kernels, fused(): pl.pallas_call(mix_kernel, out_shape=jax.ShapeDtypeStruct((8, 128, width)...  96.5 us
    unnamed x1, local copies, waits for them, and re-layouts  3.08 us

profile of v6, /device:TPU:0, one launch (start us, length us, event | category | flops | bytes accessed | tf_op | source)
XLA Modules:
  0.0 99.5 jit_solution(7736069296066118066)
XLA Ops:
  0.0 96.5 %fused.1 = bf16[8,128,1024]{2,1,0:T(8,128)(2,1)} custom-call(bf16[8,128,1024]{2,1,0:T(8,128)(2,1)} %bitcast.7, bf16[1024,1024]{1,0:T(8,128)(2,1)} %keys_hbm.1, f32[1,1024]{1,0:T(1,128)} %bitcast.8, f32[1,1024]{1,0:T(1,128)} %bitcast.9, bf16[2,1024,512]{2,1,0:T(8,128)(2,1)} %win_hbm.1, bf16[2,512,1024]{2,1,0:T(8,128)(2,1)} %wout_hbm.1, f32[7,7,1024]{2,1,0:T(8,128)} %cw_ref.1, ...), custom_call_target="tpu_custom_call" | custom-call | tf_op jit(solution)/shard_map/fused/pallas_call | solution.py:478
  96.5 3.1 %copy.12 = bf16[1,8,128,1024]{3,2,1,0:T(8,128)(2,1)} copy(bf16[1,8,128,1024]{3,2,1,0:T(8,128)(2,1)} %bitcast.6) | data formatting | bytes 4194304
